TPU v7x, 32 devices: a whole 2x2x4 slice. The times are simulated.
32 devices in a mesh: blk: 8 (over y, x, core), grp: 4 (over z).
Axes of the slice: x: 2, y: 2, z: 4, core: 2. Of those that a mesh axis runs over, the one named last changes fastest.
Arguments:
- image_tokens: float32 [128, 49, 256], P(('blk', 'grp')), may hold values from -256 to 256
- text_tokens: float32 [128, 32, 256], P('blk'), may hold values from -4 to 4
- labels: int32 [128], P(('blk', 'grp')), may hold values from 0 to 127, each once
Outputs:
- loss_total: float32 [], replicated
- image_grads: float32 [128, 49, 256], P(('blk', 'grp'))
- text_grads: float32 [128, 32, 256], P('blk')
Inputs may be any that keep to these rules, and one draw needn't show every extreme that they name: `labels`: each text index appears exactly once.
All inputs are finite; a program needn't handle non-finite values.
Results may differ from a plain program's by a relative error of at most 0.0003.
Values sent between devices are 32-bit elements; how exact they have to be, the bound alone decides.
No kernel may reach another device: no remote copies, remote signals or barrier semaphores. Data moves between devices by JAX's collectives and lax.ppermute only.
A program may use at most 128 MiB of HBM per device.

v0:
```python
import jax
import jax.numpy as jnp
from jax import lax
from jax.sharding import PartitionSpec as P

HIGH = lax.Precision.HIGHEST


def pair_terms(images, texts, labels):
    scores = jnp.einsum("bid,cjd->ijbc", images, texts, precision=HIGH)
    row_max = jnp.max(scores, axis=1, keepdims=True)
    row_exp = jnp.exp(scores - row_max)
    row_sum = jnp.sum(row_exp, axis=1, keepdims=True)
    col_max = jnp.max(scores, axis=0, keepdims=True)
    col_exp = jnp.exp(scores - col_max)
    col_sum = jnp.sum(col_exp, axis=0, keepdims=True)
    image_pool = row_max[:, 0] + jnp.log(row_sum[:, 0])
    text_pool = col_max[0] + jnp.log(col_sum[0])
    pair = 0.5 * (jnp.mean(image_pool, axis=0) + jnp.mean(text_pool, axis=0))
    logit = 4.0 * pair - 20.0
    columns = jnp.arange(texts.shape[0], dtype=jnp.int32)
    sign = jnp.where(labels[:, None] == columns[None, :], 1.0, -1.0).astype(jnp.float32)
    summed = jnp.sum(jax.nn.softplus(-sign * logit))
    dpair = -2.0 * sign * jax.nn.sigmoid(-sign * logit)
    weights = row_exp / row_sum / images.shape[1] + col_exp / col_sum / texts.shape[1]
    dscore = 0.5 * dpair[None, None] * weights
    dimage = None
    dtext = None
    dimage = jnp.einsum("ijbc,cjd->bid", dscore, texts, precision=HIGH)
    dtext = jnp.einsum("ijbc,bid->cjd", dscore, images, precision=HIGH)
    return (summed, dimage, dtext)


def on_device(image_tokens, text_tokens, labels):
    n_blk = lax.axis_size("blk")
    count = image_tokens.shape[0] * n_blk * lax.axis_size("grp")
    summed, dimage, dtext = pair_terms(
        image_tokens, lax.all_gather(text_tokens, "blk", axis=0, tiled=True), labels
    )
    summed, image_grads, text_whole = (summed, dimage, dtext)
    text_rows = lax.psum_scatter(text_whole, "blk", scatter_dimension=0, tiled=True)
    text_grads = lax.psum(text_rows, "grp")
    loss_total = lax.psum(summed, ("blk", "grp")) / count
    return (loss_total, image_grads, text_grads)


def solution(mesh):
    placed = (P(("blk", "grp"), None, None), P("blk", None, None), P(("blk", "grp")))
    return jax.shard_map(
        on_device,
        mesh=mesh,
        in_specs=placed,
        out_specs=(P(), P(("blk", "grp"), None, None), P("blk", None, None)),
        check_vma=False,
    )
```

profile of v0, /device:TPU:0, one launch (start us, length us, event | category | flops | bytes accessed | tf_op | source)
XLA Modules:
  0.0 181.8 jit_solution(12251051838545468125)
XLA Ops:
  7.2 0.0 all-gather.2.cloned.1.call-start
  7.2 2.1 %copy.6 = f32[16,32,256]{2,0,1:T(8,128)} copy(f32[16,32,256]{2,1,0:T(8,128)} %param.4) | data formatting | bytes 1048576 | tf_op args[1]
  9.4 0.0 all-gather.2.cloned.1.call-update
  9.4 0.0 reduce-scatter.2.cloned.1.call-start
  9.4 40.4 %all-gather.2.cloned.1.call-done = f32[128,32,256]{2,0,1:T(8,128)} async-done(((f32[16,32,256]{2,0,1:T(8,128)}), f32[128,32,256]{2,0,1:T(8,128)}) %all-gather.2.cloned.1.call-update) | async-done | bytes 4194320 | tf_op jit(solution)/shard_map/all_gather | solution.py:38
  49.8 6.0 %bitcast_reduce_fusion.1 = (f32[49,4,128]{2,0,1:T(8,128)S(1)}, f32[128,32,4,49]{0,3,2,1:T(8,128)S(1)}) fusion(f32[4,49,256]{2,0,1:T(4,128)} %param.3, f32[128,32,256]{2,0,1:T(8,128)} %all-gather.2.cloned.1.call-done), kind=kOutput, calls=%fused_computation.7 | convolution fusion | flops 2467028480 | bytes 7706624 | tf_op jit(solution)/shard_map/bid,cjd->ijbc/dot_general | solution.py:10
  55.8 0.0 copy-start
  55.8 0.0 copy-start.2
  55.8 0.0 copy-start.1
  55.9 1.1 fusion.7
  56.9 1.0 fusion.6
  58.0 0.0 copy-done.2
  58.0 0.1 fusion.17
  58.1 0.0 copy-done
  58.1 0.0 copy-done.1
  58.1 9.3 %convolution_bitcast_fusion = f32[128,32,256]{2,0,1:T(8,128)} fusion(f32[4,49,256]{2,0,1:T(4,128)S(1)} %copy-done.1, f32[128,32,4,49]{0,3,2,1:T(8,128)S(1)} %get-tuple-element.11, f32[32,4,128]{2,1,0:T(4,128)S(1)} %fusion.6, f32[49,4,128]{2,0,1:T(8,128)S(1)} %get-tuple-element.6, f32[4,128]{1,0:T(4,128)S(1)} %get-tuple-element.8, ...), kind=kOutput, calls=%fused_computation.13 | convolution fusion | flops 2472673280 | bytes 7940096 | tf_op jit(solution)/shard_map/ijbc,bid->cjd/dot_general | solution.py:30
  67.4 0.0 reduce-scatter.2.cloned.1.call-update
  67.4 0.2 all-reduce.2.cloned.1.call-start
  67.7 0.6 fusion.16
  68.3 50.4 %reduce-scatter.2.cloned.1.call-done = f32[16,32,256]{2,0,1:T(8,128)} async-done(((f32[128,32,256]{2,0,1:T(8,128)}), f32[16,32,256]{2,0,1:T(8,128)}) %reduce-scatter.2.cloned.1.call-update) | async-done | bytes 524304 | tf_op jit(solution)/shard_map/reduce_scatter | solution.py:41
  118.7 0.0 all-reduce.2.cloned.1.call-update
  118.7 11.6 %fusion.8 = f32[4,49,256]{2,1,0:T(8,128)S(1)} fusion(f32[128,32,256]{2,0,1:T(8,128)} %all-gather.2.cloned.1.call-done, f32[128,32,4,49]{0,3,2,1:T(8,128)} %copy-done, f32[32,4,128]{2,1,0:T(4,128)S(1)} %fusion.6, f32[49,4,128]{2,0,1:T(8,128)S(1)} %get-tuple-element.6, f32[4,128]{1,0:T(4,128)S(1)} %get-tuple-element.8, ...), kind=kOutput, calls=%fused_computation.14 | convolution fusion | flops 2472673280 | bytes 7940096 | tf_op jit(solution)/shard_map/ijbc,cjd->bid/dot_general | solution.py:29
  130.3 40.2 %psum.14 = f32[]{:T(128)} all-reduce(f32[]{:T(128)} %fusion.16), channel_id=1, replica_groups=mesh['blk'=8,'grp'=4] {'blk','grp'}, use_global_device_ids=true, to_apply=%region_7.8 | all-reduce | flops 1 | bytes 8 | tf_op jit(solution)/shard_map/psum | solution.py:43
  170.6 0.8 copy.10
  172.0 0.0 all-reduce.2.cloned.1.call-done
  172.0 2.1 %copy.11 = f32[16,32,256]{2,1,0:T(8,128)} copy(f32[16,32,256]{2,0,1:T(8,128)} %all-reduce.2.cloned.1.call-done) | data formatting | bytes 1048576
  (2 shorter events, 0.1 us)
Async XLA Ops:
  7.2 42.6 %all-gather.2.cloned.1.call-start = ((), (), s32[]{:S(2)}) async-start(), calls=%async_computation.1 | async-start | bytes 4718592 | tf_op jit(solution)/shard_map/all_gather | solution.py:38
  9.4 109.3 %reduce-scatter.2.cloned.1.call-start = ((), (), s32[]{:S(2)}) async-start(), calls=%async_computation.2 | async-start | bytes 4718592 | tf_op jit(solution)/shard_map/reduce_scatter | solution.py:41
  55.8 2.3 %copy-start = (f32[128,32,4,49]{0,3,2,1:T(8,128)}, f32[128,32,4,49]{0,3,2,1:T(8,128)S(1)}, u32[]{:S(2)}) copy-start(f32[128,32,4,49]{0,3,2,1:T(8,128)S(1)} %get-tuple-element.11) | copy-start | bytes 9633796
  55.8 2.2 %copy-start.2 = (s32[4]{0:T(128)S(1)}, s32[4]{0:T(128)}, u32[]{:S(2)}) copy-start(s32[4]{0:T(128)} %param.5) | copy-start | bytes 52
  55.8 2.3 %copy-start.1 = (f32[4,49,256]{2,0,1:T(4,128)S(1)}, f32[4,49,256]{2,0,1:T(4,128)}, u32[]{:S(2)}) copy-start(f32[4,49,256]{2,0,1:T(4,128)} %param.3) | copy-start | bytes 602116
  67.4 104.6 %all-reduce.2.cloned.1.call-start = ((), (), s32[]{:S(2)}) async-start(), calls=%async_computation.3 | async-start | bytes 1048576 | tf_op jit(solution)/shard_map/psum | solution.py:42
Sparse Core Ops, SparseCore 0:
  10.4 39.2 all-gather.1
  67.6 51.0 reduce-scatter.1
  121.1 39.0 all-reduce.1
where the time goes:
time: 182 us
  waiting for transfers between devices  90.9 us (50%)
  blocking collectives  40.2 us (22%)
  matrix products  26.9 us (15%)
  between operations  15.6 us (9%)
  local copies, waits for them, and re-layouts  5.06 us (3%)
  other arithmetic  2.85 us (2%)
    reduce_scatter x1, waiting for transfers between devices, on_device(): lax.psum_scatter(text_whole, 'blk', scatter_dimension=0, tiled=True)  50.4 us
    all_gather x1, waiting for transfers between devices, on_device(): lax.all_gather(text_tokens, 'blk', axis=0, tiled=True)  40.4 us
    psum x1, blocking collectives, on_device(): loss_total = lax.psum(summed, ('blk', 'grp')) / count  40.2 us
    dot_general x1, matrix products, pair_terms(): dimage = jnp.einsum('ijbc,cjd->bid', dscore, texts, precision=HIGH)  11.6 us
    dot_general x1, matrix products, pair_terms(): dtext = jnp.einsum('ijbc,bid->cjd', dscore, images, precision=HIGH)  9.3 us
    dot_general x1, matrix products, pair_terms(): scores = jnp.einsum('bid,cjd->ijbc', images, texts, precision=HIGH)  6.02 us
    unnamed x9, local copies, waits for them, and re-layouts  5.06 us
  transfers between devices with their start and end apart: 3, of which 2 were waited for; matrix products, arithmetic and copies ran while one was open for 7% of the time, Pallas kernels for 0%

commit v1 on v0

v1 whole, which is shorter than its diff:
```python
import functools

import jax
import jax.numpy as jnp
from jax import lax
from jax.experimental import pallas as pl
from jax.experimental.pallas import tpu as pltpu
from jax.sharding import PartitionSpec as P


F32 = jnp.float32
BF16 = jnp.bfloat16
LOW = -1e30
LOG2E = 1.4426950408889634
LN2 = 0.6931471805599453


def swap(x, axis, k):
    n = lax.axis_size(axis)
    return lax.ppermute(x, axis, [(i, i ^ k) for i in range(n)])


def tree_sum(values):
    while len(values) > 1:
        values = [a + b for a, b in zip(values[::2], values[1::2])]
    return values[0]


def split(x, parts):
    out = []
    for p in range(parts):
        h = x.astype(BF16)
        out.append(h)
        if p + 1 < parts:
            x = x - h.astype(F32)
    return out


def dot_nt(a, b):
    return lax.dot_general(a, b, (((1,), (1,)), ((), ())), preferred_element_type=F32)


def dot_nn(a, b):
    return lax.dot_general(a, b, (((1,), (0,)), ((), ())), preferred_element_type=F32)


def lane_all(x, op, step):
    while step < 128:
        x = op(x, pltpu.roll(x, step, 1))
        step *= 2
    return x


def sublane_all(x, op, step):
    while step < 8:
        x = op(x, pltpu.roll(x, step, 0))
        step *= 2
    return x


def scores_of(img, t_parts):
    ih, im, il = img
    th, tm, tl = t_parts
    return (
        dot_nt(ih, th)
        + (dot_nt(ih, tm) + dot_nt(im, th))
        + (dot_nt(im, tm) + dot_nt(ih, tl) + dot_nt(il, th))
    )


def pair_math(dims, s, lab, text):
    ni, nb, nt, nc, _ = dims
    rows, (rp, width) = ni * nb, s.shape
    tiles = rp // 8
    pad = lax.broadcasted_iota(jnp.int32, (8, 1), 0) >= rows - 8 * (tiles - 1)

    def on_last(x, fill):
        if rp == rows:
            return x
        return jnp.concatenate(
            [x[: tiles - 1], jnp.where(pad, fill, x[tiles - 1])[None]], axis=0
        )

    cols = [
        on_last((s[:, k : k + 128] * LOG2E).reshape(tiles, 8, 128), LOW)
        for k in range(0, width, 128)
    ]

    def over_lanes(x, op):
        return lane_all(x.reshape(rp, 128), op, nc).reshape(tiles, 8, 128)

    row_max = over_lanes(functools.reduce(jnp.maximum, cols), jnp.maximum)
    col_max = [sublane_all(jnp.max(x, axis=0), jnp.maximum, nb) for x in cols]
    row_exp = [jnp.exp2(x - row_max) for x in cols]
    row_sum = over_lanes(functools.reduce(jnp.add, row_exp), jnp.add)
    col_exp = [jnp.exp2(x - m[None]) for x, m in zip(cols, col_max)]
    col_sum = [sublane_all(jnp.sum(x, axis=0), jnp.add, nb) for x in col_exp]
    image_pool = on_last(row_max * LN2 + jnp.log(row_sum), 0.0)
    image_pool = sublane_all(jnp.sum(image_pool, axis=0), jnp.add, nb) * (1.0 / ni)
    text_pool = functools.reduce(
        jnp.add, [m * LN2 + jnp.log(z) for m, z in zip(col_max, col_sum)]
    )
    text_pool = lane_all(text_pool, jnp.add, nc) * (1.0 / nt)
    logit = 4.0 * (0.5 * (image_pool + text_pool)) - 20.0
    sign = jnp.where(lab == text, 1.0, -1.0)
    z = -sign * logit
    e = jnp.exp(-jnp.abs(z))
    loss = jnp.maximum(z, 0.0) + jnp.log1p(e)
    dpair = -2.0 * sign * (jnp.where(z >= 0.0, 1.0, e) / (1.0 + e))
    row_w = on_last(((0.5 / ni) * dpair)[None] / row_sum, 0.0)
    ds = [
        (re * row_w + ce * ((0.5 / nt) * dpair / cz)[None]).reshape(rp, 128)
        for re, ce, cz in zip(row_exp, col_exp, col_sum)
    ]
    return jnp.concatenate(ds, axis=1), loss


def piece_kernel(dims, n_pieces, first, last, *refs):
    ni, nb, nt, nc, d = dims
    rows = ni * nb
    rp = -(-rows // 8) * 8
    half = nc // 2
    refs = list(refs)

    def take(n):
        out, refs[:] = refs[:n], refs[n:]
        return out

    (first_ref,) = take(1)
    labs, imgs = take(n_pieces), take(n_pieces)
    if first:
        texts = take(2)
    else:
        t_parts, (acc_in, loss_in) = take(3), take(2)
    dimgs = take(n_pieces)
    if last:
        acc_out, (loss_ref,) = take(2), take(1)
    else:
        acc_out, loss_ref = take(2)
    if first:
        t_parts = take(3)
    if first or last:
        o_scr = take(4)
    scrs = take(n_pieces)
    if first:
        lab_scr, img_scr, text_scr, sems = take(4)
        bring = [
            pltpu.make_async_copy(src, dst, sems.at[i])
            for i, (src, dst) in enumerate(
                [(texts[1], text_scr), (imgs[0], img_scr), (labs[0], lab_scr)]
            )
        ]
        for copy in bring:
            copy.start()
        labs, imgs = [lab_scr], [img_scr]

    if first:
        for h, t_ref in enumerate((texts[0], text_scr)):
            if h == 1:
                for copy in bring:
                    copy.wait()
            for k in range(0, d, 128):
                scr = o_scr[2 * h + k // 128]
                scr[...] = t_ref[:, k : k + 128]
        turned = jnp.concatenate(
            [
                jnp.concatenate(
                    [
                        o_scr[2 * h + k // 128][pl.ds(j, half, stride=nt), :]
                        for j in range(nt)
                        for h in range(2)
                    ],
                    axis=0,
                )
                for k in range(0, d, 128)
            ],
            axis=1,
        )
        for ref, x in zip(t_parts, split(turned, 3)):
            ref[...] = x
    tp = [ref[...] for ref in t_parts]

    img_parts, lab_tiles = [], []
    at = lax.broadcasted_iota(jnp.int32, (8, nb), 0) % nb
    pick = at == lax.broadcasted_iota(jnp.int32, (8, nb), 1)
    for scr, img_ref, lab_ref in zip(scrs, imgs, labs):
        if rp != rows:
            scr[rp - 8 :, :] = jnp.zeros((8, d), F32)
        for i in range(ni):
            scr[i * nb : (i + 1) * nb, :] = img_ref[i]
        lab = jnp.broadcast_to(lab_ref[...].astype(F32), (8, nb))
        lab = jnp.sum(jnp.where(pick, lab, 0.0), axis=1, keepdims=True)
        lab_tiles.append(lab.astype(jnp.int32))

    loss = jnp.zeros((8, 128), F32)
    acc = None if first else acc_in[...]
    scores = []
    for scr in scrs:
        parts = split(scr[...], 3)
        img_parts.append(split(scr[...].T, 2))
        scores.append(scores_of(parts, tp))
    for p in range(n_pieces):
        ds, piece_loss = pair_math(dims, scores[p], lab_tiles[p], first_ref[...])
        loss = loss + piece_loss
        wh, wl = split(ds, 2)
        th, tm, _ = tp
        dimgs[p][...] = dot_nn(wh, th) + (dot_nn(wh, tm) + dot_nn(wl, th))
        ith, itl = img_parts[p]
        dt = dot_nn(ith, wh) + (dot_nn(ith, wl) + dot_nn(itl, wh))
        acc = dt if acc is None else acc + dt
    loss = loss * (1.0 / ((8 // nb) * (128 // nc)))
    loss = loss if first else loss + loss_in[...]
    loss_ref[...] = loss
    if last:
        acc_out[0][nt * half :, :128] = loss
        acc_out[0][nt * half :, 128:] = jnp.zeros((8, d - 128), F32)
        turned = acc.T
        for h in range(2):
            for k in range(0, d, 128):
                scr = o_scr[2 * h + k // 128]
                for j in range(nt):
                    at = j * nc + h * half
                    scr[pl.ds(j, half, stride=nt), :] = turned[at : at + half, k : k + 128]
                acc_out[h][: nt * half, k : k + 128] = scr[...]
    else:
        acc_out[...] = acc


def stay(x):
    return pltpu.with_memory_space_constraint(x, pltpu.HBM)


def pieces_call(dims, text_ids, labs, imgs, texts, state, last):
    ni, nb, nt, nc, d = dims
    rp = -(-(ni * nb) // 8) * 8
    width = nt * nc
    n = len(imgs)
    first = state is None
    vmem = pl.BlockSpec(memory_space=pltpu.VMEM)
    shape = jax.ShapeDtypeStruct
    args = list(texts) if first else list(state)
    specs = [vmem] * (1 + 2 * n + len(args))
    if first:
        for at in (1, 2, 4):
            specs[at] = pl.BlockSpec(memory_space=pltpu.HBM)
        labs, imgs, args[1] = (
            [stay(labs[0])], [stay(imgs[0])], stay(args[1])
        )
    outs = [shape((rp, d), F32)] * n
    if last:
        outs += [shape((width // 2 + 8, d), F32), shape((width // 2, d), F32)]
    else:
        outs += [shape((d, width), F32)]
    outs += [shape((8, 128), F32)]
    outs += [shape((width, d), BF16)] * 3 if first else []
    scratch = [pltpu.VMEM((width // 2, 128), F32)] * 4 if first or last else []
    scratch += [pltpu.VMEM((rp, d), F32)] * n
    if first:
        scratch += [
            pltpu.VMEM((1, nb), jnp.int32),
            pltpu.VMEM((ni, nb, d), F32),
            pltpu.VMEM((width // 2, d), F32),
            pltpu.SemaphoreType.DMA((3,)),
        ]
    out = pl.pallas_call(
        functools.partial(piece_kernel, dims, n, first, last),
        out_shape=tuple(outs),
        in_specs=specs,
        out_specs=(vmem,) * len(outs),
        scratch_shapes=scratch,
        cost_estimate=pl.CostEstimate(
            flops=2 * ni * nb * width * d * 12 * n,
            bytes_accessed=8 * width * d * 4,
            transcendentals=2 * ni * nb * width * n,
        ),
        compiler_params=pltpu.CompilerParams(vmem_limit_bytes=48 * 1024 * 1024),
    )(text_ids, *labs, *imgs, *args)
    return list(out[:n]), list(out[n:])


def sum_kernel(n, *refs):
    out_ref = refs[n]
    ni, nb, _ = out_ref.shape
    for i in range(ni):
        at = slice(i * nb, (i + 1) * nb)
        out_ref[i] = tree_sum([ref[at, :] for ref in refs[:n]])


def sum_pieces(pieces, ni, nb):
    d = pieces[0].shape[1]
    return pl.pallas_call(
        functools.partial(sum_kernel, len(pieces)),
        out_shape=jax.ShapeDtypeStruct((ni, nb, d), F32),
        in_specs=[pl.BlockSpec(memory_space=pltpu.VMEM)] * len(pieces),
        out_specs=pl.BlockSpec(memory_space=pltpu.VMEM),
        compiler_params=pltpu.CompilerParams(vmem_limit_bytes=16 * 1024 * 1024),
    )(*pieces)


def CUTS(n):
    return [0, 1, 2, n]


def steps(image_tokens, text_tokens, labels):
    nb, ni, d = image_tokens.shape
    nc, nt, _ = text_tokens.shape
    n_blk, n_grp = lax.axis_size("blk"), lax.axis_size("grp")
    count = nb * n_blk * n_grp
    dims = (ni, nb, nt, 2 * nc, d)
    blk, grp = lax.axis_index("blk"), lax.axis_index("grp")
    far = list(range(2, n_blk, 2))
    order = grp_order(n_grp)

    mine = jnp.transpose(image_tokens, (1, 0, 2))
    labels = labels.reshape(1, nb)
    texts = text_tokens.reshape(nc * nt, d)
    imgs = [mine] + [swap(mine, "blk", k) for k in far]
    labs = [labels] + [swap(labels, "blk", k) for k in far]
    other = swap(texts, "blk", 1)
    lane = lax.broadcasted_iota(jnp.int32, (8, 128), 1) % (2 * nc)
    text_ids = lane % nc + nc * jnp.where(lane < nc, blk ^ 1, blk)

    state, t_parts, grads = None, None, []
    cuts = CUTS(len(imgs))
    for lo, hi in zip(cuts[:-1], cuts[1:]):
        last = hi == len(imgs)
        g, out = pieces_call(dims, text_ids, labs[lo:hi], imgs[lo:hi], (other, texts), state, last)
        grads += g
        if state is None and not last:
            t_parts = out[2:]
        state = (*t_parts, *out[:2]) if not last else out
    acc_other, acc_mine, loss = state

    recv = swap(acc_other, "blk", 1)
    shard = (acc_mine + recv[: nc * nt]).reshape(n_grp, nc // n_grp, nt, d)
    loss = loss + recv[nc * nt :, :128]
    arrived = [
        swap(lax.dynamic_index_in_dim(shard, grp ^ k, 0, False), "grp", k)
        for k in order
    ]
    total = lax.dynamic_index_in_dim(shard, grp, 0, False)
    for a in arrived:
        total = total + a
    whole = shard
    for k, a in [(k, swap(total, "grp", k)) for k in order] + [(0, total)]:
        whole = lax.dynamic_update_index_in_dim(whole, a, grp ^ k, 0)
    text_grads = whole.reshape(nc, nt, d)

    grads = grads[:1] + [swap(g, "blk", k) for k, g in zip(far, grads[1:])]
    image_grads = jnp.transpose(sum_pieces(grads, ni, nb), (1, 0, 2))

    loss = tree_sum([loss] + [swap(loss, "blk", k) for k in far])
    loss = tree_sum([loss] + [swap(loss, "grp", k) for k in range(1, n_grp)])
    return jnp.sum(loss) / count, image_grads, text_grads


def grp_order(n_grp):
    return sorted(range(1, n_grp), key=lambda k: -k)


def solution(mesh):
    placed = (P(("blk", "grp"), None, None), P("blk", None, None), P(("blk", "grp")))
    return jax.shard_map(
        steps,
        mesh=mesh,
        in_specs=placed,
        out_specs=(P(), P(("blk", "grp"), None, None), P("blk", None, None)),
        check_vma=False,
    )
```

time: 182 us -> 65.4 us (0.36)
  waiting for transfers between devices: 90.9 us -> 15.9 us
  blocking collectives: 40.2 us -> 0 us
  starting transfers between devices: 0.3 us -> 32.9 us
  matrix products: 26.9 us -> 0 us
  between operations: 15.6 us -> 2.61 us
  Pallas kernels: 0 us -> 12.2 us
  local copies, waits for them, and re-layouts: 5.06 us -> 0.88 us
  other arithmetic: 2.85 us -> 0.74 us
    reduce_scatter x1 -> x0, waiting for transfers between devices: 50.4 us -> none  [on_device(): lax.psum_scatter(text_whole, 'blk', scatter_dimension=0, tiled=True)]
    all_gather x1 -> x0, waiting for transfers between devices: 40.4 us -> none  [on_device(): lax.all_gather(text_tokens, 'blk', axis=0, tiled=True)]
    psum x1 -> x0, blocking collectives: 40.2 us -> none  [on_device(): loss_total = lax.psum(summed, ('blk', 'grp')) / count]
    ppermute x0 -> x23, starting transfers between devices: none -> 32.9 us  [swap(): return lax.ppermute(x, axis, [(i, i ^ k) for i in range(n)])]
    dot_general x3 -> x0, matrix products: 26.9 us -> none  [the longest x1 11.6 us: pair_terms(): dimage = jnp.einsum('ijbc,cjd->bid', dscore, texts, precision=HIGH)]
    ppermute x0 -> x23, waiting for transfers between devices: none -> 15.9 us  [swap(): return lax.ppermute(x, axis, [(i, i ^ k) for i in range(n)])]
    pallas_call x0 -> x4, Pallas kernels: none -> 12.2 us  [the longest x3 11.4 us: pieces_call(): pl.pallas_call(functools.partial(piece_kernel, dims, n, first, last), out...]
    unnamed x9 -> x6, local copies, waits for them, and re-layouts: 5.06 us -> 0.8 us
  transfers between devices with their start and end apart: 3 -> 23, of which waited for: 2 -> 6; matrix products, arithmetic and copies ran while one was open for 7% -> 1% of each run, Pallas kernels for 0% -> 12%
where the time goes in v1:
time: 65.4 us; the launch traced here: 65.3 us
  starting transfers between devices  32.9 us (50%)
  waiting for transfers between devices  15.9 us (24%)
  Pallas kernels  12.2 us (19%)
  between operations  2.61 us (4%)
  local copies, waits for them, and re-layouts  0.88 us (1%)
  other arithmetic  0.74 us (1%)
    ppermute x23, starting transfers between devices, swap(): return lax.ppermute(x, axis, [(i, i ^ k) for i in range(n)])  32.9 us
    ppermute x23, waiting for transfers between devices, swap(): return lax.ppermute(x, axis, [(i, i ^ k) for i in range(n)])  15.9 us
    pallas_call x3, Pallas kernels, pieces_call(): pl.pallas_call(functools.partial(piece_kernel, dims, n, first, last), out...  11.4 us
  transfers between devices with their start and end apart: 23, of which 6 were waited for; matrix products, arithmetic and copies ran while one was open for 1% of the time, Pallas kernels for 12%

profile of v1, /device:TPU:0, one launch (start us, length us, event | category | flops | bytes accessed | tf_op | source)
XLA Modules:
  0.0 65.3 jit_solution(15562727458068046265)
XLA Ops:
  0.6 0.6 collective-permute-start.4
  1.2 2.6 %collective-permute-start.6 = (f32[49,4,256]{2,1,0:T(4,128)}, f32[49,4,256]{2,1,0:T(4,128)S(1)}, u32[]{:S(2)}, u32[]{:S(2)}) collective-permute-start(f32[49,4,256]{2,1,0:T(4,128)} %bitcast.33), channel_id=1, source_target_pairs={{0,8},{4,12},{8,0},{12,4},{16,24},{20,28},{24,16},{28,20},{1,9},{5... | collective-permute-start | bytes 602120 | tf_op jit(solution)/shard_map/ppermute | solution.py:20
  3.8 1.5 %collective-permute-start.2 = (f32[49,4,256]{2,1,0:T(4,128)}, f32[49,4,256]{2,1,0:T(4,128)S(1)}, u32[]{:S(2)}, u32[]{:S(2)}) collective-permute-start(f32[49,4,256]{2,1,0:T(4,128)} %bitcast.34), channel_id=1, source_target_pairs={{0,16},{4,20},{8,24},{12,28},{16,0},{20,4},{24,8},{28,12},{1,17},{... | collective-permute-start | bytes 602120 | tf_op jit(solution)/shard_map/ppermute | solution.py:20
  5.3 1.9 %collective-permute-start.5 = (s32[1,4]{1,0:T(1,128)S(1)}, s32[1,4]{1,0:T(1,128)S(1)}, u32[]{:S(2)}, u32[]{:S(2)}) collective-permute-start(s32[1,4]{1,0:T(1,128)S(1)} %bitcast.38), channel_id=1, source_target_pairs={{0,8},{4,12},{8,0},{12,4},{16,24},{20,28},{24,16},{28,20},{1,9},{5... | collective-permute-start | bytes 56 | tf_op jit(solution)/shard_map/ppermute | solution.py:20
  7.3 1.6 %collective-permute-start = (s32[1,4]{1,0:T(1,128)S(1)}, s32[1,4]{1,0:T(1,128)S(1)}, u32[]{:S(2)}, u32[]{:S(2)}) collective-permute-start(s32[1,4]{1,0:T(1,128)S(1)} %bitcast.39), channel_id=1, source_target_pairs={{0,16},{4,20},{8,24},{12,28},{16,0},{20,4},{24,8},{28,12},{1,17},{... | collective-permute-start | bytes 56 | tf_op jit(solution)/shard_map/ppermute | solution.py:20
  8.9 4.4 %shard_map.58 = (f32[200,256]{1,0:T(8,128)S(1)}, f32[256,1024]{1,0:T(8,128)S(1)}, f32[8,128]{1,0:T(8,128)S(1)}, bf16[1024,256]{1,0:T(8,128)(2,1)S(1)}, bf16[1024...) custom-call(s32[8,128]{1,0:T(8,128)S(1)} %fusion.2.refs_0_, s32[1,4]{1,0:T(1,128)} %bitcast.37, ...), custom_call_target="tpu_custom_call" | custom-call | flops 1233125376 | bytes 8388608 | tf_op jit(solution)/shard_map/pallas_call | solution.py:265
  13.3 0.6 collective-permute-done.5.refs_1_
  13.9 2.7 %collective-permute-start.1 = (s32[1,4]{1,0:T(1,128)S(1)}, s32[1,4]{1,0:T(1,128)S(1)}, u32[]{:S(2)}, u32[]{:S(2)}) collective-permute-start(s32[1,4]{1,0:T(1,128)S(1)} %bitcast.40), channel_id=1, source_target_pairs={{0,24},{4,28},{8,16},{12,20},{16,8},{20,12},{24,0},{28,4},{1,25},{... | collective-permute-start | bytes 56 | tf_op jit(solution)/shard_map/ppermute | solution.py:20
  16.6 2.6 %shard_map.59 = (f32[200,256]{1,0:T(8,128)S(1)}, f32[256,1024]{1,0:T(8,128)S(1)}, f32[8,128]{1,0:T(8,128)S(1)}) custom-call(s32[8,128]{1,0:T(8,128)S(1)} %fusion.2.refs_0_, s32[1,4]{1,0:T(1,128)S(1)} %collective-permute-done.5.refs_1_, f32[49,4,256]{2,1,0:T(4,128)S(1)} %collective-permute-done.6.refs_2_, ...), custom_call_target="tpu_custom_call" | custom-call | flops 1233125376 | bytes 8388608 | tf_op jit(solution)/shard_map/pallas_call | solution.py:265
  19.2 4.4 %shard_map.60 = (f32[200,256]{1,0:T(8,128)S(1)}, f32[200,256]{1,0:T(8,128)S(1)}, f32[520,256]{1,0:T(8,128)S(1)}, f32[512,256]{1,0:T(8,128)S(1)}, f32[8,128]{1,0:T(8,128)S(1)}) custom-call(s32[8,128]{1,0:T(8,128)S(1)} %fusion.2.refs_0_, s32[1,4]{1,0:T(1,128)S(1)} %collective-permute-done.refs_1_, s32[1,4]{1,0:T(1,128)S(1)} %collective-permute-done.1.refs_2_, ...), custom_call_target="tpu_custom_call" | custom-call | flops 2466250752 | bytes 8388608 | tf_op jit(solution)/shard_map/pallas_call | solution.py:265
  23.6 0.1 collective-permute-start.7
  23.7 1.0 %collective-permute-start.15 = (f32[200,256]{1,0:T(8,128)S(1)}, f32[200,256]{1,0:T(8,128)S(1)}, u32[]{:S(2)}, u32[]{:S(2)}) collective-permute-start(f32[200,256]{1,0:T(8,128)S(1)} %get-tuple-element.28), channel_id=1, source_target_pairs={{0,16},{4,20},{8,24},{12,28},{16,0},{20,4},{24,8},{28,12},{1,17},{... | collective-permute-start | bytes 614408 | tf_op jit(solution)/shard_map/ppermute | solution.py:20
  24.8 1.4 %collective-permute-start.16 = (f32[200,256]{1,0:T(8,128)S(1)}, f32[200,256]{1,0:T(8,128)S(1)}, u32[]{:S(2)}, u32[]{:S(2)}) collective-permute-start(f32[200,256]{1,0:T(8,128)S(1)} %get-tuple-element.29), channel_id=1, source_target_pairs={{0,24},{4,28},{8,16},{12,20},{16,8},{20,12},{24,0},{28,4},{1,25},{... | collective-permute-start | bytes 614408 | tf_op jit(solution)/shard_map/ppermute | solution.py:20
  26.3 3.7 %collective-permute-start.17 = (f32[4,32,256]{2,1,0:T(8,128)S(1)}, f32[4,32,256]{2,1,0:T(8,128)S(1)}, u32[]{:S(2)}, u32[]{:S(2)}) collective-permute-start(f32[4,32,256]{2,1,0:T(8,128)S(1)} %get-tuple-element.31), channel_id=1, source_target_pairs={{0,3},{1,2},{2,1},{3,0},{4,7},{5,6},{6,5},{7,4},{8,11},{9,10},{10,... | collective-permute-start | bytes 393224 | tf_op jit(solution)/shard_map/ppermute | solution.py:20
  30.0 0.8 %collective-permute-start.19 = (f32[4,32,256]{2,1,0:T(8,128)S(1)}, f32[4,32,256]{2,1,0:T(8,128)S(1)}, u32[]{:S(2)}, u32[]{:S(2)}) collective-permute-start(f32[4,32,256]{2,1,0:T(8,128)S(1)} %get-tuple-element.32), channel_id=1, source_target_pairs={{0,1},{1,0},{2,3},{3,2},{4,5},{5,4},{6,7},{7,6},{8,9},{9,8},{10,11... | collective-permute-start | bytes 393224 | tf_op jit(solution)/shard_map/ppermute | solution.py:20
  30.8 3.8 %collective-permute-done.17 = f32[4,32,256]{2,1,0:T(8,128)S(1)} collective-permute-done((f32[4,32,256]{2,1,0:T(8,128)S(1)}, f32[4,32,256]{2,1,0:T(8,128)S(1)}, u32[]{:S(2)}, u32[]{:S(2)}) %collective-permute-start.17) | collective-permute-done | bytes 131104 | tf_op jit(solution)/shard_map/ppermute | solution.py:20
  34.6 1.5 %collective-permute-start.10 = (f32[8,128]{1,0:T(8,128)S(1)}, f32[8,128]{1,0:T(8,128)S(1)}, u32[]{:S(2)}, u32[]{:S(2)}) collective-permute-start(f32[8,128]{1,0:T(8,128)S(1)} %slice_add_fusion.1), channel_id=1, source_target_pairs={{0,24},{4,28},{8,16},{12,20},{16,8},{20,12},{24,0},{28,4},{1,25},{... | collective-permute-start | bytes 12296 | tf_op jit(solution)/shard_map/ppermute | solution.py:20
  36.1 5.0 %collective-permute-done.18 = f32[4,32,256]{2,1,0:T(8,128)S(1)} collective-permute-done((f32[4,32,256]{2,1,0:T(8,128)S(1)}, f32[4,32,256]{2,1,0:T(8,128)S(1)}, u32[]{:S(2)}, u32[]{:S(2)}) %collective-permute-start.18) | collective-permute-done | bytes 131104 | tf_op jit(solution)/shard_map/ppermute | solution.py:20
  41.1 1.1 %collective-permute-start.8 = (f32[8,128]{1,0:T(8,128)S(1)}, f32[8,128]{1,0:T(8,128)S(1)}, u32[]{:S(2)}, u32[]{:S(2)}) collective-permute-start(f32[8,128]{1,0:T(8,128)S(1)} %slice_add_fusion.1), channel_id=1, source_target_pairs={{0,8},{4,12},{8,0},{12,4},{16,24},{20,28},{24,16},{28,20},{1,9},{5... | collective-permute-start | bytes 12296 | tf_op jit(solution)/shard_map/ppermute | solution.py:20
  42.2 1.0 %collective-permute-start.9 = (f32[8,128]{1,0:T(8,128)S(1)}, f32[8,128]{1,0:T(8,128)S(1)}, u32[]{:S(2)}, u32[]{:S(2)}) collective-permute-start(f32[8,128]{1,0:T(8,128)S(1)} %slice_add_fusion.1), channel_id=1, source_target_pairs={{0,16},{4,20},{8,24},{12,28},{16,0},{20,4},{24,8},{28,12},{1,17},{... | collective-permute-start | bytes 12296 | tf_op jit(solution)/shard_map/ppermute | solution.py:20
  43.2 1.4 %collective-permute-start.14 = (f32[200,256]{1,0:T(8,128)S(1)}, f32[200,256]{1,0:T(8,128)S(1)}, u32[]{:S(2)}, u32[]{:S(2)}) collective-permute-start(f32[200,256]{1,0:T(8,128)S(1)} %get-tuple-element.27), channel_id=1, source_target_pairs={{0,8},{4,12},{8,0},{12,4},{16,24},{20,28},{24,16},{28,20},{1,9},{5... | collective-permute-start | bytes 614408 | tf_op jit(solution)/shard_map/ppermute | solution.py:20
  44.7 2.5 %collective-permute-start.20 = (f32[4,32,256]{2,1,0:T(8,128)S(1)}, f32[4,32,256]{2,1,0:T(8,128)S(1)}, u32[]{:S(2)}, u32[]{:S(2)}) collective-permute-start(f32[4,32,256]{2,1,0:T(8,128)S(1)} %fusion.1), channel_id=1, source_target_pairs={{0,3},{1,2},{2,1},{3,0},{4,7},{5,6},{6,5},{7,4},{8,11},{9,10},{10,... | collective-permute-start | bytes 393224 | tf_op jit(solution)/shard_map/ppermute | solution.py:20
  47.3 1.9 %collective-permute-start.12 = (f32[8,128]{1,0:T(8,128)S(1)}, f32[8,128]{1,0:T(8,128)S(1)}, u32[]{:S(2)}, u32[]{:S(2)}) collective-permute-start(f32[8,128]{1,0:T(8,128)S(1)} %add_add_fusion), channel_id=1, source_target_pairs={{0,2},{1,3},{2,0},{3,1},{4,6},{5,7},{6,4},{7,5},{8,10},{9,11},{10,... | collective-permute-start | bytes 12296 | tf_op jit(solution)/shard_map/ppermute | solution.py:20
  49.2 2.5 %collective-permute-start.13 = (f32[8,128]{1,0:T(8,128)S(1)}, f32[8,128]{1,0:T(8,128)S(1)}, u32[]{:S(2)}, u32[]{:S(2)}) collective-permute-start(f32[8,128]{1,0:T(8,128)S(1)} %add_add_fusion), channel_id=1, source_target_pairs={{0,3},{1,2},{2,1},{3,0},{4,7},{5,6},{6,5},{7,4},{8,11},{9,10},{10,... | collective-permute-start | bytes 12296 | tf_op jit(solution)/shard_map/ppermute | solution.py:20
  51.7 0.8 %shard_map.61 = f32[49,4,256]{2,1,0:T(4,128)} custom-call(f32[200,256]{1,0:T(8,128)S(1)} %get-tuple-element.26.refs_0_, f32[200,256]{1,0:T(8,128)S(1)} %collective-permute-done.14.refs_1_, f32[200,256]{1,0:T(8,128)S(1)} %collective-permute-done.15.refs_2_, f32[200,256]{1,0:T(8,128)S(1)} %collective-permute-done.16.refs_3_), custom_call_target="tpu_custom_call" | custom-call | tf_op jit(solution)/shard_map/pallas_call | solution.py:291
  52.4 2.2 %collective-permute-done.13 = f32[8,128]{1,0:T(8,128)S(1)} collective-permute-done((f32[8,128]{1,0:T(8,128)S(1)}, f32[8,128]{1,0:T(8,128)S(1)}, u32[]{:S(2)}, u32[]{:S(2)}) %collective-permute-start.13) | collective-permute-done | bytes 4128 | tf_op jit(solution)/shard_map/ppermute | solution.py:20
  54.6 0.6 add_reduce_fusion
  55.8 0.1 collective-permute-start.21
  55.9 3.0 %collective-permute-start.22 = (f32[4,32,256]{2,1,0:T(8,128)S(1)}, f32[4,32,256]{2,1,0:T(8,128)S(1)}, u32[]{:S(2)}, u32[]{:S(2)}) collective-permute-start(f32[4,32,256]{2,1,0:T(8,128)S(1)} %fusion.1), channel_id=1, source_target_pairs={{0,1},{1,0},{2,3},{3,2},{4,5},{5,4},{6,7},{7,6},{8,9},{9,8},{10,11... | collective-permute-start | bytes 393224 | tf_op jit(solution)/shard_map/ppermute | solution.py:20
  59.0 3.9 %collective-permute-done.21 = f32[4,32,256]{2,1,0:T(8,128)S(1)} collective-permute-done((f32[4,32,256]{2,1,0:T(8,128)S(1)}, f32[4,32,256]{2,1,0:T(8,128)S(1)}, u32[]{:S(2)}, u32[]{:S(2)}) %collective-permute-start.21) | collective-permute-done | bytes 131104 | tf_op jit(solution)/shard_map/ppermute | solution.py:20
  62.9 0.4 collective-permute-done.22
  63.3 0.8 %copy-done = f32[4,4,32,256]{3,2,1,0:T(8,128)} copy-done((f32[4,4,32,256]{3,2,1,0:T(8,128)}, f32[4,4,32,256]{3,2,1,0:T(8,128)S(1)}, u32[]{:S(2)}) %copy-start) | copy-done | bytes 524312
  (37 shorter events, 0.4 us)
Async XLA Ops:
  0.6 6.7 %collective-permute-start.4 = (f32[512,256]{1,0:T(8,128)}, f32[512,256]{1,0:T(8,128)S(1)}, u32[]{:S(2)}, u32[]{:S(2)}) collective-permute-start(f32[512,256]{1,0:T(8,128)} %bitcast.31), channel_id=1, source_target_pairs={{0,4},{4,0},{8,12},{12,8},{16,20},{20,16},{24,28},{28,24},{1,5},{5... | collective-permute-start | bytes 1572872 | tf_op jit(solution)/shard_map/ppermute | solution.py:20
  1.2 4.1 %copy-start.1 = (s32[4]{0:T(128)S(1)}, s32[4]{0:T(128)}, u32[]{:S(2)}) copy-start(s32[4]{0:T(128)} %param.5) | copy-start | bytes 52
  1.2 15.4 %collective-permute-start.6 = (f32[49,4,256]{2,1,0:T(4,128)}, f32[49,4,256]{2,1,0:T(4,128)S(1)}, u32[]{:S(2)}, u32[]{:S(2)}) collective-permute-start(f32[49,4,256]{2,1,0:T(4,128)} %bitcast.33), channel_id=1, source_target_pairs={{0,8},{4,12},{8,0},{12,4},{16,24},{20,28},{24,16},{28,20},{1,9},{5... | collective-permute-start | bytes 602120 | tf_op jit(solution)/shard_map/ppermute | solution.py:20
  3.8 15.4 %collective-permute-start.2 = (f32[49,4,256]{2,1,0:T(4,128)}, f32[49,4,256]{2,1,0:T(4,128)S(1)}, u32[]{:S(2)}, u32[]{:S(2)}) collective-permute-start(f32[49,4,256]{2,1,0:T(4,128)} %bitcast.34), channel_id=1, source_target_pairs={{0,16},{4,20},{8,24},{12,28},{16,0},{20,4},{24,8},{28,12},{1,17},{... | collective-permute-start | bytes 602120 | tf_op jit(solution)/shard_map/ppermute | solution.py:20
  5.3 13.9 %collective-permute-start.3 = (f32[49,4,256]{2,1,0:T(4,128)}, f32[49,4,256]{2,1,0:T(4,128)S(1)}, u32[]{:S(2)}, u32[]{:S(2)}) collective-permute-start(f32[49,4,256]{2,1,0:T(4,128)} %bitcast.35), channel_id=1, source_target_pairs={{0,24},{4,28},{8,16},{12,20},{16,8},{20,12},{24,0},{28,4},{1,25},{... | collective-permute-start | bytes 602120 | tf_op jit(solution)/shard_map/ppermute | solution.py:20
  5.3 8.6 %collective-permute-start.5 = (s32[1,4]{1,0:T(1,128)S(1)}, s32[1,4]{1,0:T(1,128)S(1)}, u32[]{:S(2)}, u32[]{:S(2)}) collective-permute-start(s32[1,4]{1,0:T(1,128)S(1)} %bitcast.38), channel_id=1, source_target_pairs={{0,8},{4,12},{8,0},{12,4},{16,24},{20,28},{24,16},{28,20},{1,9},{5... | collective-permute-start | bytes 56 | tf_op jit(solution)/shard_map/ppermute | solution.py:20
  7.3 6.6 %copy-start.2 = (s32[4]{0:T(128)S(1)}, s32[4]{0:T(128)}, u32[]{:S(2)}) copy-start(s32[4]{0:T(128)} %param.5) | copy-start | bytes 52
  7.3 11.9 %collective-permute-start = (s32[1,4]{1,0:T(1,128)S(1)}, s32[1,4]{1,0:T(1,128)S(1)}, u32[]{:S(2)}, u32[]{:S(2)}) collective-permute-start(s32[1,4]{1,0:T(1,128)S(1)} %bitcast.39), channel_id=1, source_target_pairs={{0,16},{4,20},{8,24},{12,28},{16,0},{20,4},{24,8},{28,12},{1,17},{... | collective-permute-start | bytes 56 | tf_op jit(solution)/shard_map/ppermute | solution.py:20
  13.9 5.3 %collective-permute-start.1 = (s32[1,4]{1,0:T(1,128)S(1)}, s32[1,4]{1,0:T(1,128)S(1)}, u32[]{:S(2)}, u32[]{:S(2)}) collective-permute-start(s32[1,4]{1,0:T(1,128)S(1)} %bitcast.40), channel_id=1, source_target_pairs={{0,24},{4,28},{8,16},{12,20},{16,8},{20,12},{24,0},{28,4},{1,25},{... | collective-permute-start | bytes 56 | tf_op jit(solution)/shard_map/ppermute | solution.py:20
  23.6 2.5 %collective-permute-start.7 = (f32[520,256]{1,0:T(8,128)S(1)}, f32[520,256]{1,0:T(8,128)S(1)}, u32[]{:S(2)}, u32[]{:S(2)}) collective-permute-start(f32[520,256]{1,0:T(8,128)S(1)} %get-tuple-element.25), channel_id=1, source_target_pairs={{0,4},{4,0},{8,12},{12,8},{16,20},{20,16},{24,28},{28,24},{1,5},{5... | collective-permute-start | bytes 1597448 | tf_op jit(solution)/shard_map/ppermute | solution.py:20
  23.7 23.5 %collective-permute-start.15 = (f32[200,256]{1,0:T(8,128)S(1)}, f32[200,256]{1,0:T(8,128)S(1)}, u32[]{:S(2)}, u32[]{:S(2)}) collective-permute-start(f32[200,256]{1,0:T(8,128)S(1)} %get-tuple-element.28), channel_id=1, source_target_pairs={{0,16},{4,20},{8,24},{12,28},{16,0},{20,4},{24,8},{28,12},{1,17},{... | collective-permute-start | bytes 614408 | tf_op jit(solution)/shard_map/ppermute | solution.py:20
  24.8 24.4 %collective-permute-start.16 = (f32[200,256]{1,0:T(8,128)S(1)}, f32[200,256]{1,0:T(8,128)S(1)}, u32[]{:S(2)}, u32[]{:S(2)}) collective-permute-start(f32[200,256]{1,0:T(8,128)S(1)} %get-tuple-element.29), channel_id=1, source_target_pairs={{0,24},{4,28},{8,16},{12,20},{16,8},{20,12},{24,0},{28,4},{1,25},{... | collective-permute-start | bytes 614408 | tf_op jit(solution)/shard_map/ppermute | solution.py:20
  26.3 8.3 %collective-permute-start.17 = (f32[4,32,256]{2,1,0:T(8,128)S(1)}, f32[4,32,256]{2,1,0:T(8,128)S(1)}, u32[]{:S(2)}, u32[]{:S(2)}) collective-permute-start(f32[4,32,256]{2,1,0:T(8,128)S(1)} %get-tuple-element.31), channel_id=1, source_target_pairs={{0,3},{1,2},{2,1},{3,0},{4,7},{5,6},{6,5},{7,4},{8,11},{9,10},{10,... | collective-permute-start | bytes 393224 | tf_op jit(solution)/shard_map/ppermute | solution.py:20
  30.0 11.1 %collective-permute-start.18 = (f32[4,32,256]{2,1,0:T(8,128)S(1)}, f32[4,32,256]{2,1,0:T(8,128)S(1)}, u32[]{:S(2)}, u32[]{:S(2)}) collective-permute-start(f32[4,32,256]{2,1,0:T(8,128)S(1)} %get-tuple-element.33), channel_id=1, source_target_pairs={{0,2},{1,3},{2,0},{3,1},{4,6},{5,7},{6,4},{7,5},{8,10},{9,11},{10,... | collective-permute-start | bytes 393224 | tf_op jit(solution)/shard_map/ppermute | solution.py:20
  30.0 12.2 %collective-permute-start.19 = (f32[4,32,256]{2,1,0:T(8,128)S(1)}, f32[4,32,256]{2,1,0:T(8,128)S(1)}, u32[]{:S(2)}, u32[]{:S(2)}) collective-permute-start(f32[4,32,256]{2,1,0:T(8,128)S(1)} %get-tuple-element.32), channel_id=1, source_target_pairs={{0,1},{1,0},{2,3},{3,2},{4,5},{5,4},{6,7},{7,6},{8,9},{9,8},{10,11... | collective-permute-start | bytes 393224 | tf_op jit(solution)/shard_map/ppermute | solution.py:20
  34.6 8.6 %collective-permute-start.10 = (f32[8,128]{1,0:T(8,128)S(1)}, f32[8,128]{1,0:T(8,128)S(1)}, u32[]{:S(2)}, u32[]{:S(2)}) collective-permute-start(f32[8,128]{1,0:T(8,128)S(1)} %slice_add_fusion.1), channel_id=1, source_target_pairs={{0,24},{4,28},{8,16},{12,20},{16,8},{20,12},{24,0},{28,4},{1,25},{... | collective-permute-start | bytes 12296 | tf_op jit(solution)/shard_map/ppermute | solution.py:20
  41.1 3.6 %collective-permute-start.8 = (f32[8,128]{1,0:T(8,128)S(1)}, f32[8,128]{1,0:T(8,128)S(1)}, u32[]{:S(2)}, u32[]{:S(2)}) collective-permute-start(f32[8,128]{1,0:T(8,128)S(1)} %slice_add_fusion.1), channel_id=1, source_target_pairs={{0,8},{4,12},{8,0},{12,4},{16,24},{20,28},{24,16},{28,20},{1,9},{5... | collective-permute-start | bytes 12296 | tf_op jit(solution)/shard_map/ppermute | solution.py:20
  42.2 5.0 %collective-permute-start.9 = (f32[8,128]{1,0:T(8,128)S(1)}, f32[8,128]{1,0:T(8,128)S(1)}, u32[]{:S(2)}, u32[]{:S(2)}) collective-permute-start(f32[8,128]{1,0:T(8,128)S(1)} %slice_add_fusion.1), channel_id=1, source_target_pairs={{0,16},{4,20},{8,24},{12,28},{16,0},{20,4},{24,8},{28,12},{1,17},{... | collective-permute-start | bytes 12296 | tf_op jit(solution)/shard_map/ppermute | solution.py:20
  43.2 8.4 %collective-permute-start.14 = (f32[200,256]{1,0:T(8,128)S(1)}, f32[200,256]{1,0:T(8,128)S(1)}, u32[]{:S(2)}, u32[]{:S(2)}) collective-permute-start(f32[200,256]{1,0:T(8,128)S(1)} %get-tuple-element.27), channel_id=1, source_target_pairs={{0,8},{4,12},{8,0},{12,4},{16,24},{20,28},{24,16},{28,20},{1,9},{5... | collective-permute-start | bytes 614408 | tf_op jit(solution)/shard_map/ppermute | solution.py:20
  44.7 14.2 %collective-permute-start.20 = (f32[4,32,256]{2,1,0:T(8,128)S(1)}, f32[4,32,256]{2,1,0:T(8,128)S(1)}, u32[]{:S(2)}, u32[]{:S(2)}) collective-permute-start(f32[4,32,256]{2,1,0:T(8,128)S(1)} %fusion.1), channel_id=1, source_target_pairs={{0,3},{1,2},{2,1},{3,0},{4,7},{5,6},{6,5},{7,4},{8,11},{9,10},{10,... | collective-permute-start | bytes 393224 | tf_op jit(solution)/shard_map/ppermute | solution.py:20
  47.2 5.2 %collective-permute-start.11 = (f32[8,128]{1,0:T(8,128)S(1)}, f32[8,128]{1,0:T(8,128)S(1)}, u32[]{:S(2)}, u32[]{:S(2)}) collective-permute-start(f32[8,128]{1,0:T(8,128)S(1)} %add_add_fusion), channel_id=1, source_target_pairs={{0,1},{1,0},{2,3},{3,2},{4,5},{5,4},{6,7},{7,6},{8,9},{9,8},{10,11... | collective-permute-start | bytes 12296 | tf_op jit(solution)/shard_map/ppermute | solution.py:20
  47.3 5.1 %collective-permute-start.12 = (f32[8,128]{1,0:T(8,128)S(1)}, f32[8,128]{1,0:T(8,128)S(1)}, u32[]{:S(2)}, u32[]{:S(2)}) collective-permute-start(f32[8,128]{1,0:T(8,128)S(1)} %add_add_fusion), channel_id=1, source_target_pairs={{0,2},{1,3},{2,0},{3,1},{4,6},{5,7},{6,4},{7,5},{8,10},{9,11},{10,... | collective-permute-start | bytes 12296 | tf_op jit(solution)/shard_map/ppermute | solution.py:20
  49.2 5.4 %collective-permute-start.13 = (f32[8,128]{1,0:T(8,128)S(1)}, f32[8,128]{1,0:T(8,128)S(1)}, u32[]{:S(2)}, u32[]{:S(2)}) collective-permute-start(f32[8,128]{1,0:T(8,128)S(1)} %add_add_fusion), channel_id=1, source_target_pairs={{0,3},{1,2},{2,1},{3,0},{4,7},{5,6},{6,5},{7,4},{8,11},{9,10},{10,... | collective-permute-start | bytes 12296 | tf_op jit(solution)/shard_map/ppermute | solution.py:20
  55.8 7.0 %collective-permute-start.21 = (f32[4,32,256]{2,1,0:T(8,128)S(1)}, f32[4,32,256]{2,1,0:T(8,128)S(1)}, u32[]{:S(2)}, u32[]{:S(2)}) collective-permute-start(f32[4,32,256]{2,1,0:T(8,128)S(1)} %fusion.1), channel_id=1, source_target_pairs={{0,2},{1,3},{2,0},{3,1},{4,6},{5,7},{6,4},{7,5},{8,10},{9,11},{10,... | collective-permute-start | bytes 393224 | tf_op jit(solution)/shard_map/ppermute | solution.py:20
  55.9 7.4 %collective-permute-start.22 = (f32[4,32,256]{2,1,0:T(8,128)S(1)}, f32[4,32,256]{2,1,0:T(8,128)S(1)}, u32[]{:S(2)}, u32[]{:S(2)}) collective-permute-start(f32[4,32,256]{2,1,0:T(8,128)S(1)} %fusion.1), channel_id=1, source_target_pairs={{0,1},{1,0},{2,3},{3,2},{4,5},{5,4},{6,7},{7,6},{8,9},{9,8},{10,11... | collective-permute-start | bytes 393224 | tf_op jit(solution)/shard_map/ppermute | solution.py:20
  63.3 0.8 %copy-start = (f32[4,4,32,256]{3,2,1,0:T(8,128)}, f32[4,4,32,256]{3,2,1,0:T(8,128)S(1)}, u32[]{:S(2)}) copy-start(f32[4,4,32,256]{3,2,1,0:T(8,128)S(1)} %bitcast_dynamic-update-slice_fusion) | copy-start | bytes 1572868

commit v2 on v0

v2 whole, which is shorter than its diff:
```python
import functools

import jax
import jax.numpy as jnp
from jax import lax
from jax.experimental import pallas as pl
from jax.experimental.pallas import tpu as pltpu
from jax.sharding import PartitionSpec as P


F32 = jnp.float32
BF16 = jnp.bfloat16
LOW = -1e30
LOG2E = 1.4426950408889634
LN2 = 0.6931471805599453
MIB = 1024 * 1024


def ORDER(n):
    return sorted(range(1, n), key=lambda k: -k)


def swap(x, axis, k):
    n = lax.axis_size(axis)
    return lax.ppermute(x, axis, [(i, i ^ k) for i in range(n)])


def tree_sum(values):
    while len(values) > 1:
        values = [a + b for a, b in zip(values[::2], values[1::2])]
    return values[0]


def split(x, parts):
    out = []
    for p in range(parts):
        h = x.astype(BF16)
        out.append(h)
        if p + 1 < parts:
            x = x - h.astype(F32)
    return out


def dot_nt(a, b):
    return lax.dot_general(a, b, (((1,), (1,)), ((), ())), preferred_element_type=F32)


def dot_nn(a, b):
    return lax.dot_general(a, b, (((1,), (0,)), ((), ())), preferred_element_type=F32)


def lane_all(x, op, step):
    while step < 128:
        x = op(x, pltpu.roll(x, step, 1))
        step *= 2
    return x


def sublane_all(x, op, step):
    while step < 8:
        x = op(x, pltpu.roll(x, step, 0))
        step *= 2
    return x


def stay(x):
    return pltpu.with_memory_space_constraint(x, pltpu.HBM)


def specs(n):
    return [pl.BlockSpec(memory_space=pltpu.VMEM)] * n


def scores_of(img, t_parts):
    ih, im, il = img
    th, tm, tl = t_parts
    return (
        dot_nt(ih, th)
        + (dot_nt(ih, tm) + dot_nt(im, th))
        + (dot_nt(im, tm) + dot_nt(ih, tl) + dot_nt(il, th))
    )


def pair_math(dims, s, lab, text):
    ni, nb, nt, nc, _ = dims
    rows, (rp, width) = ni * nb, s.shape
    tiles = rp // 8
    pad = lax.broadcasted_iota(jnp.int32, (8, 1), 0) >= rows - 8 * (tiles - 1)

    def on_last(x, fill):
        if rp == rows:
            return x
        return jnp.concatenate(
            [x[: tiles - 1], jnp.where(pad, fill, x[tiles - 1])[None]], axis=0
        )

    cols = [
        on_last((s[:, k : k + 128] * LOG2E).reshape(tiles, 8, 128), LOW)
        for k in range(0, width, 128)
    ]

    def over_lanes(x, op):
        return lane_all(x.reshape(rp, 128), op, nc).reshape(tiles, 8, 128)

    row_max = over_lanes(functools.reduce(jnp.maximum, cols), jnp.maximum)
    col_max = [sublane_all(jnp.max(x, axis=0), jnp.maximum, nb) for x in cols]
    row_exp = [jnp.exp2(x - row_max) for x in cols]
    row_sum = over_lanes(functools.reduce(jnp.add, row_exp), jnp.add)
    col_exp = [jnp.exp2(x - m[None]) for x, m in zip(cols, col_max)]
    col_sum = [sublane_all(jnp.sum(x, axis=0), jnp.add, nb) for x in col_exp]
    image_pool = on_last(row_max * LN2 + jnp.log(row_sum), 0.0)
    image_pool = sublane_all(jnp.sum(image_pool, axis=0), jnp.add, nb) * (1.0 / ni)
    text_pool = functools.reduce(
        jnp.add, [m * LN2 + jnp.log(z) for m, z in zip(col_max, col_sum)]
    )
    text_pool = lane_all(text_pool, jnp.add, nc) * (1.0 / nt)
    logit = 4.0 * (0.5 * (image_pool + text_pool)) - 20.0
    sign = jnp.where(lab == text, 1.0, -1.0)
    z = -sign * logit
    e = jnp.exp(-jnp.abs(z))
    loss = jnp.maximum(z, 0.0) + jnp.log1p(e)
    dpair = -2.0 * sign * (jnp.where(z >= 0.0, 1.0, e) / (1.0 + e))
    row_w = on_last(((0.5 / ni) * dpair)[None] / row_sum, 0.0)
    ds = [
        (re * row_w + ce * ((0.5 / nt) * dpair / cz)[None]).reshape(rp, 128)
        for re, ce, cz in zip(row_exp, col_exp, col_sum)
    ]
    return jnp.concatenate(ds, axis=1), loss * (1.0 / ((8 // nb) * (128 // nc)))


def label_tile(img_ref, nb):
    rp = img_ref.shape[0]
    tail = img_ref[rp - 8 :, :128]
    sub = lax.broadcasted_iota(jnp.int32, (8, 128), 0)
    return jnp.where(sub >= 8 - nb, tail, pltpu.roll(tail, nb, 0)).astype(jnp.int32)


def image_grad(w, t_parts):
    wh, wl = w
    th, tm, _ = t_parts
    return dot_nn(wh, th) + (dot_nn(wh, tm) + dot_nn(wl, th))


def text_grad(turned_img, w):
    (ith, itl), (wh, wl) = turned_img, w
    return dot_nn(ith, wh) + (dot_nn(ith, wl) + dot_nn(itl, wh))


def weights_of(dims, imgs, t_parts, text):
    scores, turned, out, losses = [], [], [], []
    for ref in imgs:
        img = ref[...]
        turned.append(split(img.T, 2))
        scores.append(scores_of(split(img, 3), t_parts))
    for ref, s in zip(imgs, scores):
        ds, loss = pair_math(dims, s, label_tile(ref, dims[1]), text)
        out.append(split(ds, 2))
        losses.append(loss)
    return turned, out, functools.reduce(jnp.add, losses)


def first_kernel(dims, ids_ref, img_ref, other_ref, own_ref, *refs):
    _, _, nt, nc, _ = dims
    half = nc // 2
    dimg_ref, acc_ref, loss_ref, *t_refs = refs[:6]
    scrs = refs[6:]
    for k, scr in enumerate(scrs):
        scr[...] = other_ref[:, 128 * k : 128 * (k + 1)]
    text = jnp.concatenate(
        [
            jnp.concatenate(
                [
                    x
                    for j in range(nt)
                    for x in (
                        scr[pl.ds(j, half, stride=nt), :],
                        own_ref[j * half : (j + 1) * half, 128 * k : 128 * (k + 1)],
                    )
                ],
                axis=0,
            )
            for k, scr in enumerate(scrs)
        ],
        axis=1,
    )
    for ref, x in zip(t_refs, split(text, 3)):
        ref[...] = x
    tp = [ref[...] for ref in t_refs]
    turned, w, loss = weights_of(dims, [img_ref], tp, ids_ref[...])
    loss_ref[...] = loss
    dimg_ref[...] = image_grad(w[0], tp)
    acc_ref[...] = text_grad(turned[0], w[0])


def middle_kernel(dims, n, ids_ref, *refs):
    imgs, (acc_in, loss_in, *t_refs) = refs[:n], refs[n : n + 5]
    dimgs, (acc_ref, loss_ref) = refs[n + 5 : 2 * n + 5], refs[2 * n + 5 :]
    tp = [ref[...] for ref in t_refs]
    turned, w, loss = weights_of(dims, imgs, tp, ids_ref[...])
    loss_ref[...] = loss_in[...] + loss
    acc = acc_in[...]
    for p in range(n):
        dimgs[p][...] = image_grad(w[p], tp)
        acc = acc + text_grad(turned[p], w[p])
    acc_ref[...] = acc


def hand_out(dims, turned, send_ref, own_ref):
    nt, nc, d = dims[2:]
    half = nc // 2
    for j in range(nt):
        g, q = divmod(j, 8)
        for k in range(d // 128):
            to = ((g * (d // 128) + k) * 8 + q) * half
            for h, ref in enumerate((send_ref, own_ref)):
                ref[to : to + half, :] = turned[
                    j * nc + h * half : j * nc + (h + 1) * half,
                    128 * k : 128 * (k + 1),
                ]


def last_kernel(dims, n, ids_ref, *refs):
    imgs, (acc_in, loss_in, *t_refs) = refs[:n], refs[n : n + 5]
    send_ref, own_ref, *keep = refs[n + 5 :]
    tp = [ref[...] for ref in t_refs]
    turned, w, loss = weights_of(dims, imgs, tp, ids_ref[...])
    acc = acc_in[...]
    for p in range(n):
        acc = acc + text_grad(turned[p], w[p])
        for ref, x in zip(keep[2 * p : 2 * p + 2], w[p]):
            ref[...] = x
    hand_out(dims, acc.T, send_ref, own_ref)
    for ref in (send_ref, own_ref):
        ref[ref.shape[0] - 8 :, :] = loss_in[...] + loss


def rest_kernel(n, th_ref, tm_ref, *refs):
    tp = (th_ref[...], tm_ref[...], None)
    for p in range(n):
        w = [ref[...] for ref in refs[2 * p : 2 * p + 2]]
        refs[2 * n + p][...] = image_grad(w, tp)


def call(kernel, outs, args, dims, n, mats, scratch=(), limit=48):
    ni, nb, nt, nc, d = dims
    return pl.pallas_call(
        kernel,
        out_shape=tuple(jax.ShapeDtypeStruct(*o) for o in outs),
        in_specs=specs(len(args)),
        out_specs=tuple(specs(len(outs))),
        scratch_shapes=list(scratch),
        cost_estimate=pl.CostEstimate(
            flops=2 * ni * nb * nt * nc * d * mats * n,
            bytes_accessed=4 * nt * nc * d,
            transcendentals=2 * ni * nb * nt * nc * n,
        ),
        compiler_params=pltpu.CompilerParams(vmem_limit_bytes=limit * MIB),
    )(*args)


def compute(dims, ids, imgs, other, own):
    ni, nb, nt, nc, d = dims
    width = nt * nc
    rp = ni * nb + nb
    part = (nt * nc * d // 2 // 128 + 8, 128)
    img, acc, loss = ((rp, d), F32), ((d, width), F32), ((8, 128), F32)
    keep = [((rp, width), BF16)] * 2
    dimgs = []
    out = call(
        functools.partial(first_kernel, dims),
        [img, acc, loss] + [((width, d), BF16)] * 3,
        [ids, imgs[0], other, own],
        dims,
        1,
        12,
        [pltpu.VMEM((width // 2, 128), F32)] * (d // 128),
    )
    dimgs.append(out[0])
    state, t_parts = out[1:3], out[3:]
    n_last = 2 if len(imgs) > 2 else 1
    for p in range(1, len(imgs) - n_last):
        *g, a, b = call(
            functools.partial(middle_kernel, dims, 1),
            [img, acc, loss],
            [ids, imgs[p], *state, *t_parts],
            dims,
            1,
            12,
        )
        dimgs += g
        state = (a, b)
    send, own, *kept = call(
        functools.partial(last_kernel, dims, n_last),
        [(part, F32)] * 2 + keep * n_last,
        [ids, *imgs[-n_last:], *state, *t_parts],
        dims,
        n_last,
        9,
    )
    g = call(
        functools.partial(rest_kernel, n_last),
        [img] * n_last,
        [*t_parts[:2], *kept],
        dims,
        n_last,
        3,
    )
    return dimgs + list(g), send, own


def pack_kernel(lab_hbm, img_hbm, out_ref, lab_scr, img_scr, sems):
    ni, nb, d = img_scr.shape
    bring = [
        pltpu.make_async_copy(img_hbm, img_scr, sems.at[0]),
        pltpu.make_async_copy(lab_hbm, lab_scr, sems.at[1]),
    ]
    for copy in bring:
        copy.start()
    for copy in bring:
        copy.wait()
    for i in range(ni):
        out_ref[i * nb : (i + 1) * nb, :] = img_scr[i]
    across = lax.broadcasted_iota(jnp.int32, (nb, nb), 0)
    along = lax.broadcasted_iota(jnp.int32, (nb, nb), 1)
    lab = jnp.broadcast_to(lab_scr[...].astype(F32), (nb, nb))
    lab = jnp.sum(jnp.where(across == along, lab, 0.0), axis=1, keepdims=True)
    out_ref[ni * nb :, :] = jnp.broadcast_to(lab, (nb, d))


def pack(images, labels):
    ni, nb, d = images.shape
    return pl.pallas_call(
        pack_kernel,
        out_shape=jax.ShapeDtypeStruct((ni * nb + nb, d), F32),
        in_specs=[pl.BlockSpec(memory_space=pltpu.HBM)] * 2,
        out_specs=pl.BlockSpec(memory_space=pltpu.VMEM),
        scratch_shapes=[
            pltpu.VMEM((1, nb), jnp.int32),
            pltpu.VMEM((ni, nb, d), F32),
            pltpu.SemaphoreType.DMA((2,)),
        ],
        compiler_params=pltpu.CompilerParams(vmem_limit_bytes=8 * MIB),
    )(stay(labels.reshape(1, nb)), stay(images))


def turn_kernel(nt, text_hbm, out_ref, *refs):
    *scrs, sems = refs
    half = scrs[0].shape[0] // nt
    bring = [
        pltpu.make_async_copy(
            text_hbm.at[:, pl.ds(128 * k, 128)], scr, sems.at[k]
        )
        for k, scr in enumerate(scrs)
    ]
    for copy in bring:
        copy.start()
    for k, scr in enumerate(scrs):
        bring[k].wait()
        for j in range(nt):
            out_ref[j * half : (j + 1) * half, 128 * k : 128 * (k + 1)] = scr[
                pl.ds(j, half, stride=nt), :
            ]


def turn(texts, nt):
    rows, d = texts.shape
    return pl.pallas_call(
        functools.partial(turn_kernel, nt),
        out_shape=jax.ShapeDtypeStruct((rows, d), F32),
        in_specs=[pl.BlockSpec(memory_space=pltpu.HBM)],
        out_specs=pl.BlockSpec(memory_space=pltpu.VMEM),
        scratch_shapes=[pltpu.VMEM((rows, 128), F32)] * (d // 128)
        + [pltpu.SemaphoreType.DMA((d // 128,))],
        compiler_params=pltpu.CompilerParams(vmem_limit_bytes=8 * MIB),
    )(stay(texts))


def sum_kernel(n, *refs):
    out_ref = refs[n]
    ni, nb, _ = out_ref.shape
    for i in range(ni):
        at = slice(i * nb, (i + 1) * nb)
        out_ref[i] = tree_sum([ref[at, :] for ref in refs[:n]])


def sum_pieces(pieces, ni, nb):
    d = pieces[0].shape[1]
    return pl.pallas_call(
        functools.partial(sum_kernel, len(pieces)),
        out_shape=jax.ShapeDtypeStruct((ni, nb, d), F32),
        in_specs=specs(len(pieces)),
        out_specs=specs(1)[0],
        compiler_params=pltpu.CompilerParams(vmem_limit_bytes=16 * MIB),
    )(*pieces)


def merge_kernel(n, own_ref, recv_ref, *outs):
    rows = outs[0].shape[0] - 8
    grp = lax.axis_index("grp")
    loss = own_ref[n * rows :, :] + recv_ref[n * rows :, :]
    for k, ref in enumerate(outs):
        at = pl.ds(pl.multiple_of((grp ^ k) * rows, 8), rows)
        ref[:rows, :] = own_ref[at, :] + recv_ref[at, :]
        ref[rows:, :] = loss


def merge(own, recv, n):
    rows = (own.shape[0] - 8) // n + 8
    return pl.pallas_call(
        functools.partial(merge_kernel, n),
        out_shape=(jax.ShapeDtypeStruct((rows, 128), F32),) * n,
        in_specs=specs(2),
        out_specs=tuple(specs(n)),
        compiler_params=pltpu.CompilerParams(vmem_limit_bytes=16 * MIB),
    )(own, recv)


def place_kernel(n, *refs):
    ranks, out_ref = refs[:n], refs[n]
    nc, nt, d = out_ref.shape
    lanes = d // 128
    units = nt // 8 * lanes // n
    grp = lax.axis_index("grp")
    for s in range(n):
        for i in range(units):
            unit = (grp ^ s) * units + i
            row = pl.multiple_of(8 * (unit // lanes), 8)
            lane = pl.multiple_of(128 * (unit % lanes), 128)
            for c in range(nc):
                out_ref[c, pl.ds(row, 8), pl.ds(lane, 128)] = ranks[s][
                    pl.ds(8 * nc * i + c, 8, stride=nc), :
                ]


def place(ranks, shape):
    return pl.pallas_call(
        functools.partial(place_kernel, len(ranks)),
        out_shape=jax.ShapeDtypeStruct(shape, F32),
        in_specs=specs(len(ranks)),
        out_specs=specs(1)[0],
        compiler_params=pltpu.CompilerParams(vmem_limit_bytes=16 * MIB),
    )(*ranks)


def steps(image_tokens, text_tokens, labels):
    nb, ni, d = image_tokens.shape
    nc, nt, _ = text_tokens.shape
    n_blk, n_grp = lax.axis_size("blk"), lax.axis_size("grp")
    count = nb * n_blk * n_grp
    dims = (ni, nb, nt, 2 * nc, d)
    blk = lax.axis_index("blk")
    far = list(range(2, n_blk, 2))
    order = grp_order(n_grp)

    mine = pack(jnp.transpose(image_tokens, (1, 0, 2)), labels)
    texts = text_tokens.reshape(nc * nt, d)
    imgs = [mine] + [swap(mine, "blk", k) for k in far]
    other = swap(texts, "blk", 1)
    own = turn(texts, nt)
    lane = lax.broadcasted_iota(jnp.int32, (8, 128), 1) % (2 * nc)
    text_ids = lane % nc + nc * jnp.where(lane < nc, blk ^ 1, blk)

    grads, send, own_part = compute(dims, text_ids, imgs, other, own)

    parts = merge(own_part, swap(send, "blk", 1), n_grp)
    arrived = {k: swap(parts[k], "grp", k) for k in order}
    total = tree_sum([parts[0]] + [arrived[k] for k in range(1, n_grp)])
    rows = total.shape[0] - 8
    total, loss = total[:rows], total[rows:]
    got = {k: swap(total, "grp", k) for k in order}
    text_grads = place([total] + [got[k] for k in range(1, n_grp)], (nc, nt, d))

    grads = grads[:1] + [swap(g, "blk", k) for k, g in zip(far, grads[1:])]
    image_grads = jnp.transpose(sum_pieces(grads, ni, nb), (1, 0, 2))

    parts = [loss] + [swap(loss, "blk", k) for k in far]
    loss = jnp.sum(tree_sum(parts)) / count
    return loss, image_grads, text_grads


def grp_order(n_grp):
    return ORDER(n_grp)


def solution(mesh):
    placed = (P(("blk", "grp"), None, None), P("blk", None, None), P(("blk", "grp")))
    return jax.shard_map(
        steps,
        mesh=mesh,
        in_specs=placed,
        out_specs=(P(), P(("blk", "grp"), None, None), P("blk", None, None)),
        check_vma=False,
    )
```

time: 182 us -> 54.2 us (0.30)
  waiting for transfers between devices: 90.9 us -> 15.1 us
  blocking collectives: 40.2 us -> 0 us
  matrix products: 26.9 us -> 0 us
  starting transfers between devices: 0.3 us -> 21.6 us
  Pallas kernels: 0 us -> 14.2 us
  between operations: 15.6 us -> 2.51 us
  local copies, waits for them, and re-layouts: 5.06 us -> 0.01 us
  other arithmetic: 2.85 us -> 0.66 us
    reduce_scatter x1 -> x0, waiting for transfers between devices: 50.4 us -> none  [on_device(): lax.psum_scatter(text_whole, 'blk', scatter_dimension=0, tiled=True)]
    all_gather x1 -> x0, waiting for transfers between devices: 40.4 us -> none  [on_device(): lax.all_gather(text_tokens, 'blk', axis=0, tiled=True)]
    psum x1 -> x0, blocking collectives: 40.2 us -> none  [on_device(): loss_total = lax.psum(summed, ('blk', 'grp')) / count]
    dot_general x3 -> x0, matrix products: 26.9 us -> none  [the longest x1 11.6 us: pair_terms(): dimage = jnp.einsum('ijbc,cjd->bid', dscore, texts, precision=HIGH)]
    ppermute x0 -> x17, starting transfers between devices: none -> 21.6 us  [swap(): return lax.ppermute(x, axis, [(i, i ^ k) for i in range(n)])]
    ppermute x0 -> x17, waiting for transfers between devices: none -> 15.1 us  [swap(): return lax.ppermute(x, axis, [(i, i ^ k) for i in range(n)])]
    pallas_call x0 -> x9, Pallas kernels: none -> 14.2 us  [the longest x4 10 us: call(): pl.pallas_call(kernel, out_shape=tuple((jax.ShapeDtypeStruct(*o) for o in...]
    unnamed x9 -> x0, local copies, waits for them, and re-layouts: 5.06 us -> none
  transfers between devices with their start and end apart: 3 -> 17, of which waited for: 2 -> 9; matrix products, arithmetic and copies ran while one was open for 7% -> 1% of each run, Pallas kernels for 0% -> 17%
where the time goes in v2:
time: 54.2 us; the launch traced here: 54 us
  starting transfers between devices  21.6 us (40%)
  waiting for transfers between devices  15.1 us (28%)
  Pallas kernels  14.2 us (26%)
  between operations  2.51 us (5%)
  other arithmetic  0.66 us (1%)
    ppermute x17, starting transfers between devices, swap(): return lax.ppermute(x, axis, [(i, i ^ k) for i in range(n)])  21.6 us
    ppermute x17, waiting for transfers between devices, swap(): return lax.ppermute(x, axis, [(i, i ^ k) for i in range(n)])  15.1 us
    pallas_call x4, Pallas kernels, call(): pl.pallas_call(kernel, out_shape=tuple((jax.ShapeDtypeStruct(*o) for o in...  10 us
    pallas_call x1, Pallas kernels, turn(): pl.pallas_call(functools.partial(turn_kernel, nt), out_shape=jax.ShapeDty...  1.28 us
  transfers between devices with their start and end apart: 17, of which 9 were waited for; matrix products, arithmetic and copies ran while one was open for 1% of the time, Pallas kernels for 17%

profile of v2, /device:TPU:0, one launch (start us, length us, event | category | flops | bytes accessed | tf_op | source)
XLA Modules:
  0.0 54.0 jit_solution(11633801833878348525)
XLA Ops:
  0.6 0.6 %collective-permute-start.3 = (f32[512,256]{1,0:T(8,128)}, f32[512,256]{1,0:T(8,128)S(1)}, u32[]{:S(2)}, u32[]{:S(2)}) collective-permute-start(f32[512,256]{1,0:T(8,128)} %bitcast.4), channel_id=1, source_target_pairs={{0,4},{4,0},{8,12},{12,8},{16,20},{20,16},{24,28},{28,24},{1,5},{5... | collective-permute-start | bytes 1572872 | tf_op jit(solution)/shard_map/ppermute | solution.py:25
  1.2 1.0 %shard_map.58.img_ref = f32[200,256]{1,0:T(8,128)S(1)} custom-call(s32[1,4]{1,0:T(1,128)} %bitcast.8, f32[49,4,256]{2,1,0:T(4,128)} %bitcast.6), custom_call_target="tpu_custom_call" | custom-call | tf_op jit(solution)/shard_map/pallas_call | solution.py:332
  2.2 2.6 %collective-permute-start.2 = (f32[200,256]{1,0:T(8,128)S(1)}, f32[200,256]{1,0:T(8,128)S(1)}, u32[]{:S(2)}, u32[]{:S(2)}) collective-permute-start(f32[200,256]{1,0:T(8,128)S(1)} %shard_map.58.img_ref), channel_id=1, source_target_pairs={{0,8},{4,12},{8,0},{12,4},{16,24},{20,28},{24,16},{28,20},{1,9},{5... | collective-permute-start | bytes 614408 | tf_op jit(solution)/shard_map/ppermute | solution.py:25
  4.8 1.5 %collective-permute-start.1 = (f32[200,256]{1,0:T(8,128)S(1)}, f32[200,256]{1,0:T(8,128)S(1)}, u32[]{:S(2)}, u32[]{:S(2)}) collective-permute-start(f32[200,256]{1,0:T(8,128)S(1)} %shard_map.58.img_ref), channel_id=1, source_target_pairs={{0,24},{4,28},{8,16},{12,20},{16,8},{20,12},{24,0},{28,4},{1,25},{... | collective-permute-start | bytes 614408 | tf_op jit(solution)/shard_map/ppermute | solution.py:25
  6.4 1.3 %shard_map.59.own_ref = f32[512,256]{1,0:T(8,128)S(1)} custom-call(f32[512,256]{1,0:T(8,128)} %bitcast.5), custom_call_target="tpu_custom_call" | custom-call | tf_op jit(solution)/shard_map/pallas_call | solution.py:367
  7.7 2.9 %shard_map.60 = (f32[200,256]{1,0:T(8,128)S(1)}, f32[256,1024]{1,0:T(8,128)S(1)}, f32[8,128]{1,0:T(8,128)S(1)}, bf16[1024,256]{1,0:T(8,128)(2,1)S(1)}, bf16[1024...) custom-call(s32[8,128]{1,0:T(8,128)S(1)} %fusion.ids_ref, f32[200,256]{1,0:T(8,128)S(1)} %shard_map.58.img_ref, ...), custom_call_target="tpu_custom_call" | custom-call | flops 1233125376 | bytes 1048576 | tf_op jit(solution)/shard_map/pallas_call | solution.py:246
  10.7 2.6 %shard_map.61 = (f32[200,256]{1,0:T(8,128)S(1)}, f32[256,1024]{1,0:T(8,128)S(1)}, f32[8,128]{1,0:T(8,128)S(1)}) custom-call(s32[8,128]{1,0:T(8,128)S(1)} %fusion.ids_ref, f32[200,256]{1,0:T(8,128)S(1)} %collective-permute-done.2.refs_0_, f32[256,1024]{1,0:T(8,128)S(1)} %get-tuple-element.24.refs_1_, f32[8,128]{1,0:T(8,128)S(1)} %get-tuple-element.25.refs_2_, ...), custom_call_target="tpu_custom_call" | custom-call | flops 1233125376 | bytes 1048576 | tf_op jit(solution)/shard_map/pallas_call | solution.py:246
  13.3 2.9 %collective-permute-done.1.refs_1_ = f32[200,256]{1,0:T(8,128)S(1)} collective-permute-done((f32[200,256]{1,0:T(8,128)S(1)}, f32[200,256]{1,0:T(8,128)S(1)}, u32[]{:S(2)}, u32[]{:S(2)}) %collective-permute-start.1) | collective-permute-done | bytes 204832 | tf_op jit(solution)/shard_map/ppermute | solution.py:25
  16.2 1.4 %collective-permute-done.refs_0_ = f32[200,256]{1,0:T(8,128)S(1)} collective-permute-done((f32[200,256]{1,0:T(8,128)S(1)}, f32[200,256]{1,0:T(8,128)S(1)}, u32[]{:S(2)}, u32[]{:S(2)}) %collective-permute-start) | collective-permute-done | bytes 204832 | tf_op jit(solution)/shard_map/ppermute | solution.py:25
  17.6 3.7 %shard_map.62 = (f32[1032,128]{1,0:T(8,128)S(1)}, f32[1032,128]{1,0:T(8,128)S(1)}, bf16[200,1024]{1,0:T(8,128)(2,1)S(1)}, bf16[200,1024]{1,0:T(8,128)(2,1)S(1)},...) custom-call(s32[8,128]{1,0:T(8,128)S(1)} %fusion.ids_ref, f32[200,256]{1,0:T(8,128)S(1)} %collective-permute-done.refs_0_, ...), custom_call_target="tpu_custom_call" | custom-call | flops 1849688064 | bytes 1048576 | tf_op jit(solution)/shard_map/pallas_call | solution.py:246
  21.3 1.9 %collective-permute-done.4.recv_ref = f32[1032,128]{1,0:T(8,128)S(1)} collective-permute-done((f32[1032,128]{1,0:T(8,128)S(1)}, f32[1032,128]{1,0:T(8,128)S(1)}, u32[]{:S(2)}, u32[]{:S(2)}) %collective-permute-start.4) | collective-permute-done | bytes 528416 | tf_op jit(solution)/shard_map/ppermute | solution.py:25
  23.3 1.6 %collective-permute-start.5 = (f32[264,128]{1,0:T(8,128)S(1)}, f32[264,128]{1,0:T(8,128)S(1)}, u32[]{:S(2)}, u32[]{:S(2)}) collective-permute-start(f32[264,128]{1,0:T(8,128)S(1)} %get-tuple-element.34), channel_id=1, source_target_pairs={{0,1},{1,0},{2,3},{3,2},{4,5},{5,4},{6,7},{7,6},{8,9},{9,8},{10,11... | collective-permute-start | bytes 405512 | tf_op jit(solution)/shard_map/ppermute | solution.py:25
  25.0 2.6 %collective-permute-start.6 = (f32[264,128]{1,0:T(8,128)S(1)}, f32[264,128]{1,0:T(8,128)S(1)}, u32[]{:S(2)}, u32[]{:S(2)}) collective-permute-start(f32[264,128]{1,0:T(8,128)S(1)} %get-tuple-element.35), channel_id=1, source_target_pairs={{0,2},{1,3},{2,0},{3,1},{4,6},{5,7},{6,4},{7,5},{8,10},{9,11},{10,... | collective-permute-start | bytes 405512 | tf_op jit(solution)/shard_map/ppermute | solution.py:25
  27.6 0.2 collective-permute-start.7
  27.8 1.5 %collective-permute-start.11 = (f32[200,256]{1,0:T(8,128)S(1)}, f32[200,256]{1,0:T(8,128)S(1)}, u32[]{:S(2)}, u32[]{:S(2)}) collective-permute-start(f32[200,256]{1,0:T(8,128)S(1)} %get-tuple-element.38), channel_id=1, source_target_pairs={{0,8},{4,12},{8,0},{12,4},{16,24},{20,28},{24,16},{28,20},{1,9},{5... | collective-permute-start | bytes 614408 | tf_op jit(solution)/shard_map/ppermute | solution.py:25
  29.3 0.8 %shard_map.64 = (f32[200,256]{1,0:T(8,128)S(1)}, f32[200,256]{1,0:T(8,128)S(1)}) custom-call(bf16[1024,256]{1,0:T(8,128)(2,1)S(1)} %get-tuple-element.26.refs_3_.refs_4_.th_ref, bf16[1024,256]{1,0:T(8,128)(2,1)S(1)} %get-tuple-element.27.refs_4_.refs_5_.tm_ref, bf16[200,1024]{1,0:T(8,128)(2,1)S(1)} %get-tuple-element.39.refs_0_, ...), custom_call_target="tpu_custom_call" | custom-call | flops 616562688 | bytes 1048576 | tf_op jit(solution)/shard_map/pallas_call | solution.py:246
  30.1 0.6 %collective-permute-start.12 = (f32[200,256]{1,0:T(8,128)S(1)}, f32[200,256]{1,0:T(8,128)S(1)}, u32[]{:S(2)}, u32[]{:S(2)}) collective-permute-start(f32[200,256]{1,0:T(8,128)S(1)} %get-tuple-element.43), channel_id=1, source_target_pairs={{0,16},{4,20},{8,24},{12,28},{16,0},{20,4},{24,8},{28,12},{1,17},{... | collective-permute-start | bytes 614408 | tf_op jit(solution)/shard_map/ppermute | solution.py:25
  30.7 0.4 collective-permute-done.5
  31.1 1.4 %collective-permute-start.13 = (f32[200,256]{1,0:T(8,128)S(1)}, f32[200,256]{1,0:T(8,128)S(1)}, u32[]{:S(2)}, u32[]{:S(2)}) collective-permute-start(f32[200,256]{1,0:T(8,128)S(1)} %get-tuple-element.44), channel_id=1, source_target_pairs={{0,24},{4,28},{8,16},{12,20},{16,8},{20,12},{24,0},{28,4},{1,25},{... | collective-permute-start | bytes 614408 | tf_op jit(solution)/shard_map/ppermute | solution.py:25
  32.5 5.6 %collective-permute-done.6 = f32[264,128]{1,0:T(8,128)S(1)} collective-permute-done((f32[264,128]{1,0:T(8,128)S(1)}, f32[264,128]{1,0:T(8,128)S(1)}, u32[]{:S(2)}, u32[]{:S(2)}) %collective-permute-start.6) | collective-permute-done | bytes 135200 | tf_op jit(solution)/shard_map/ppermute | solution.py:25
  38.2 2.5 %collective-permute-start.16 = (f32[256,128]{1,0:T(8,128)S(1)}, f32[256,128]{1,0:T(8,128)S(1)}, u32[]{:S(2)}, u32[]{:S(2)}) collective-permute-start(f32[256,128]{1,0:T(8,128)S(1)} %slice.9.refs_0_), channel_id=1, source_target_pairs={{0,3},{1,2},{2,1},{3,0},{4,7},{5,6},{6,5},{7,4},{8,11},{9,10},{10,... | collective-permute-start | bytes 393224 | tf_op jit(solution)/shard_map/ppermute | solution.py:25
  40.7 1.4 %collective-permute-start.15 = (f32[256,128]{1,0:T(8,128)S(1)}, f32[256,128]{1,0:T(8,128)S(1)}, u32[]{:S(2)}, u32[]{:S(2)}) collective-permute-start(f32[256,128]{1,0:T(8,128)S(1)} %slice.9.refs_0_), channel_id=1, source_target_pairs={{0,2},{1,3},{2,0},{3,1},{4,6},{5,7},{6,4},{7,5},{8,10},{9,11},{10,... | collective-permute-start | bytes 393224 | tf_op jit(solution)/shard_map/ppermute | solution.py:25
  42.1 0.5 collective-permute-start.14
  42.6 0.5 collective-permute-start.9
  43.2 2.5 %collective-permute-start.10 = (f32[8,128]{1,0:T(8,128)S(1)}, f32[8,128]{1,0:T(8,128)S(1)}, u32[]{:S(2)}, u32[]{:S(2)}) collective-permute-start(f32[8,128]{1,0:T(8,128)S(1)} %slice.8), channel_id=1, source_target_pairs={{0,24},{4,28},{8,16},{12,20},{16,8},{20,12},{24,0},{28,4},{1,25},{... | collective-permute-start | bytes 12296 | tf_op jit(solution)/shard_map/ppermute | solution.py:25
  45.6 0.6 %collective-permute-done.9 = f32[8,128]{1,0:T(8,128)S(1)} collective-permute-done((f32[8,128]{1,0:T(8,128)S(1)}, f32[8,128]{1,0:T(8,128)S(1)}, u32[]{:S(2)}, u32[]{:S(2)}) %collective-permute-start.9) | collective-permute-done | bytes 4128 | tf_op jit(solution)/shard_map/ppermute | solution.py:25
  46.2 1.5 %collective-permute-start.8 = (f32[8,128]{1,0:T(8,128)S(1)}, f32[8,128]{1,0:T(8,128)S(1)}, u32[]{:S(2)}, u32[]{:S(2)}) collective-permute-start(f32[8,128]{1,0:T(8,128)S(1)} %slice.8), channel_id=1, source_target_pairs={{0,8},{4,12},{8,0},{12,4},{16,24},{20,28},{24,16},{28,20},{1,9},{5... | collective-permute-start | bytes 12296 | tf_op jit(solution)/shard_map/ppermute | solution.py:25
  47.7 0.8 %shard_map.65 = f32[49,4,256]{2,1,0:T(4,128)} custom-call(f32[200,256]{1,0:T(8,128)S(1)} %get-tuple-element.37.refs_0_, f32[200,256]{1,0:T(8,128)S(1)} %collective-permute-done.11.refs_1_, f32[200,256]{1,0:T(8,128)S(1)} %collective-permute-done.12.refs_2_, f32[200,256]{1,0:T(8,128)S(1)} %collective-permute-done.13.refs_3_), custom_call_target="tpu_custom_call" | custom-call | tf_op jit(solution)/shard_map/pallas_call | solution.py:388
  48.5 1.3 %collective-permute-done.8 = f32[8,128]{1,0:T(8,128)S(1)} collective-permute-done((f32[8,128]{1,0:T(8,128)S(1)}, f32[8,128]{1,0:T(8,128)S(1)}, u32[]{:S(2)}, u32[]{:S(2)}) %collective-permute-start.8) | collective-permute-done | bytes 4128 | tf_op jit(solution)/shard_map/ppermute | solution.py:25
  49.9 0.6 %add_reduce_fusion = f32[]{:T(128)} fusion(f32[8,128]{1,0:T(8,128)S(1)} %collective-permute-done.9, f32[8,128]{1,0:T(8,128)S(1)} %collective-permute-done.10, f32[8,128]{1,0:T(8,128)S(1)} %collective-permute-done.8, f32[264,128]{1,0:T(8,128)S(1)} %add_add_fusion), kind=kLoop, calls=%fused_computation.9 | loop fusion | flops 4095 | bytes 16388 | tf_op jit(solution)/shard_map/reduce_sum | solution.py:477
  51.1 0.8 %collective-permute-done.15.refs_2_ = f32[256,128]{1,0:T(8,128)S(1)} collective-permute-done((f32[256,128]{1,0:T(8,128)S(1)}, f32[256,128]{1,0:T(8,128)S(1)}, u32[]{:S(2)}, u32[]{:S(2)}) %collective-permute-start.15) | collective-permute-done | bytes 131104 | tf_op jit(solution)/shard_map/ppermute | solution.py:25
  51.9 1.0 %shard_map.66 = f32[16,32,256]{2,1,0:T(8,128)} custom-call(f32[256,128]{1,0:T(8,128)S(1)} %slice.9.refs_0_, f32[256,128]{1,0:T(8,128)S(1)} %collective-permute-done.14.refs_1_, f32[256,128]{1,0:T(8,128)S(1)} %collective-permute-done.15.refs_2_, f32[256,128]{1,0:T(8,128)S(1)} %collective-permute-done.16.refs_3_), custom_call_target="tpu_custom_call" | custom-call | tf_op jit(solution)/shard_map/pallas_call | solution.py:436
  (18 shorter events, 0.4 us)
Async XLA Ops:
  0.6 7.0 %collective-permute-start.3 = (f32[512,256]{1,0:T(8,128)}, f32[512,256]{1,0:T(8,128)S(1)}, u32[]{:S(2)}, u32[]{:S(2)}) collective-permute-start(f32[512,256]{1,0:T(8,128)} %bitcast.4), channel_id=1, source_target_pairs={{0,4},{4,0},{8,12},{12,8},{16,20},{20,16},{24,28},{28,24},{1,5},{5... | collective-permute-start | bytes 1572872 | tf_op jit(solution)/shard_map/ppermute | solution.py:25
  2.2 8.5 %collective-permute-start.2 = (f32[200,256]{1,0:T(8,128)S(1)}, f32[200,256]{1,0:T(8,128)S(1)}, u32[]{:S(2)}, u32[]{:S(2)}) collective-permute-start(f32[200,256]{1,0:T(8,128)S(1)} %shard_map.58.img_ref), channel_id=1, source_target_pairs={{0,8},{4,12},{8,0},{12,4},{16,24},{20,28},{24,16},{28,20},{1,9},{5... | collective-permute-start | bytes 614408 | tf_op jit(solution)/shard_map/ppermute | solution.py:25
  4.8 11.4 %collective-permute-start.1 = (f32[200,256]{1,0:T(8,128)S(1)}, f32[200,256]{1,0:T(8,128)S(1)}, u32[]{:S(2)}, u32[]{:S(2)}) collective-permute-start(f32[200,256]{1,0:T(8,128)S(1)} %shard_map.58.img_ref), channel_id=1, source_target_pairs={{0,24},{4,28},{8,16},{12,20},{16,8},{20,12},{24,0},{28,4},{1,25},{... | collective-permute-start | bytes 614408 | tf_op jit(solution)/shard_map/ppermute | solution.py:25
  6.3 11.3 %collective-permute-start = (f32[200,256]{1,0:T(8,128)S(1)}, f32[200,256]{1,0:T(8,128)S(1)}, u32[]{:S(2)}, u32[]{:S(2)}) collective-permute-start(f32[200,256]{1,0:T(8,128)S(1)} %shard_map.58.img_ref), channel_id=1, source_target_pairs={{0,16},{4,20},{8,24},{12,28},{16,0},{20,4},{24,8},{28,12},{1,17},{... | collective-permute-start | bytes 614408 | tf_op jit(solution)/shard_map/ppermute | solution.py:25
  21.3 2.0 %collective-permute-start.4 = (f32[1032,128]{1,0:T(8,128)S(1)}, f32[1032,128]{1,0:T(8,128)S(1)}, u32[]{:S(2)}, u32[]{:S(2)}) collective-permute-start(f32[1032,128]{1,0:T(8,128)S(1)} %get-tuple-element.32), channel_id=1, source_target_pairs={{0,4},{4,0},{8,12},{12,8},{16,20},{20,16},{24,28},{28,24},{1,5},{5... | collective-permute-start | bytes 1585160 | tf_op jit(solution)/shard_map/ppermute | solution.py:25
  23.3 7.7 %collective-permute-start.5 = (f32[264,128]{1,0:T(8,128)S(1)}, f32[264,128]{1,0:T(8,128)S(1)}, u32[]{:S(2)}, u32[]{:S(2)}) collective-permute-start(f32[264,128]{1,0:T(8,128)S(1)} %get-tuple-element.34), channel_id=1, source_target_pairs={{0,1},{1,0},{2,3},{3,2},{4,5},{5,4},{6,7},{7,6},{8,9},{9,8},{10,11... | collective-permute-start | bytes 405512 | tf_op jit(solution)/shard_map/ppermute | solution.py:25
  25.0 13.1 %collective-permute-start.6 = (f32[264,128]{1,0:T(8,128)S(1)}, f32[264,128]{1,0:T(8,128)S(1)}, u32[]{:S(2)}, u32[]{:S(2)}) collective-permute-start(f32[264,128]{1,0:T(8,128)S(1)} %get-tuple-element.35), channel_id=1, source_target_pairs={{0,2},{1,3},{2,0},{3,1},{4,6},{5,7},{6,4},{7,5},{8,10},{9,11},{10,... | collective-permute-start | bytes 405512 | tf_op jit(solution)/shard_map/ppermute | solution.py:25
  27.6 10.6 %collective-permute-start.7 = (f32[264,128]{1,0:T(8,128)S(1)}, f32[264,128]{1,0:T(8,128)S(1)}, u32[]{:S(2)}, u32[]{:S(2)}) collective-permute-start(f32[264,128]{1,0:T(8,128)S(1)} %get-tuple-element.36), channel_id=1, source_target_pairs={{0,3},{1,2},{2,1},{3,0},{4,7},{5,6},{6,5},{7,4},{8,11},{9,10},{10,... | collective-permute-start | bytes 405512 | tf_op jit(solution)/shard_map/ppermute | solution.py:25
  27.8 14.3 %collective-permute-start.11 = (f32[200,256]{1,0:T(8,128)S(1)}, f32[200,256]{1,0:T(8,128)S(1)}, u32[]{:S(2)}, u32[]{:S(2)}) collective-permute-start(f32[200,256]{1,0:T(8,128)S(1)} %get-tuple-element.38), channel_id=1, source_target_pairs={{0,8},{4,12},{8,0},{12,4},{16,24},{20,28},{24,16},{28,20},{1,9},{5... | collective-permute-start | bytes 614408 | tf_op jit(solution)/shard_map/ppermute | solution.py:25
  30.1 12.5 %collective-permute-start.12 = (f32[200,256]{1,0:T(8,128)S(1)}, f32[200,256]{1,0:T(8,128)S(1)}, u32[]{:S(2)}, u32[]{:S(2)}) collective-permute-start(f32[200,256]{1,0:T(8,128)S(1)} %get-tuple-element.43), channel_id=1, source_target_pairs={{0,16},{4,20},{8,24},{12,28},{16,0},{20,4},{24,8},{28,12},{1,17},{... | collective-permute-start | bytes 614408 | tf_op jit(solution)/shard_map/ppermute | solution.py:25
  31.1 12.1 %collective-permute-start.13 = (f32[200,256]{1,0:T(8,128)S(1)}, f32[200,256]{1,0:T(8,128)S(1)}, u32[]{:S(2)}, u32[]{:S(2)}) collective-permute-start(f32[200,256]{1,0:T(8,128)S(1)} %get-tuple-element.44), channel_id=1, source_target_pairs={{0,24},{4,28},{8,16},{12,20},{16,8},{20,12},{24,0},{28,4},{1,25},{... | collective-permute-start | bytes 614408 | tf_op jit(solution)/shard_map/ppermute | solution.py:25
  38.2 12.9 %collective-permute-start.16 = (f32[256,128]{1,0:T(8,128)S(1)}, f32[256,128]{1,0:T(8,128)S(1)}, u32[]{:S(2)}, u32[]{:S(2)}) collective-permute-start(f32[256,128]{1,0:T(8,128)S(1)} %slice.9.refs_0_), channel_id=1, source_target_pairs={{0,3},{1,2},{2,1},{3,0},{4,7},{5,6},{6,5},{7,4},{8,11},{9,10},{10,... | collective-permute-start | bytes 393224 | tf_op jit(solution)/shard_map/ppermute | solution.py:25
  40.7 11.2 %collective-permute-start.15 = (f32[256,128]{1,0:T(8,128)S(1)}, f32[256,128]{1,0:T(8,128)S(1)}, u32[]{:S(2)}, u32[]{:S(2)}) collective-permute-start(f32[256,128]{1,0:T(8,128)S(1)} %slice.9.refs_0_), channel_id=1, source_target_pairs={{0,2},{1,3},{2,0},{3,1},{4,6},{5,7},{6,4},{7,5},{8,10},{9,11},{10,... | collective-permute-start | bytes 393224 | tf_op jit(solution)/shard_map/ppermute | solution.py:25
  42.1 9.8 %collective-permute-start.14 = (f32[256,128]{1,0:T(8,128)S(1)}, f32[256,128]{1,0:T(8,128)S(1)}, u32[]{:S(2)}, u32[]{:S(2)}) collective-permute-start(f32[256,128]{1,0:T(8,128)S(1)} %slice.9.refs_0_), channel_id=1, source_target_pairs={{0,1},{1,0},{2,3},{3,2},{4,5},{5,4},{6,7},{7,6},{8,9},{9,8},{10,11... | collective-permute-start | bytes 393224 | tf_op jit(solution)/shard_map/ppermute | solution.py:25
  42.6 3.6 %collective-permute-start.9 = (f32[8,128]{1,0:T(8,128)S(1)}, f32[8,128]{1,0:T(8,128)S(1)}, u32[]{:S(2)}, u32[]{:S(2)}) collective-permute-start(f32[8,128]{1,0:T(8,128)S(1)} %slice.8), channel_id=1, source_target_pairs={{0,16},{4,20},{8,24},{12,28},{16,0},{20,4},{24,8},{28,12},{1,17},{... | collective-permute-start | bytes 12296 | tf_op jit(solution)/shard_map/ppermute | solution.py:25
  43.2 5.4 %collective-permute-start.10 = (f32[8,128]{1,0:T(8,128)S(1)}, f32[8,128]{1,0:T(8,128)S(1)}, u32[]{:S(2)}, u32[]{:S(2)}) collective-permute-start(f32[8,128]{1,0:T(8,128)S(1)} %slice.8), channel_id=1, source_target_pairs={{0,24},{4,28},{8,16},{12,20},{16,8},{20,12},{24,0},{28,4},{1,25},{... | collective-permute-start | bytes 12296 | tf_op jit(solution)/shard_map/ppermute | solution.py:25
  46.2 3.6 %collective-permute-start.8 = (f32[8,128]{1,0:T(8,128)S(1)}, f32[8,128]{1,0:T(8,128)S(1)}, u32[]{:S(2)}, u32[]{:S(2)}) collective-permute-start(f32[8,128]{1,0:T(8,128)S(1)} %slice.8), channel_id=1, source_target_pairs={{0,8},{4,12},{8,0},{12,4},{16,24},{20,28},{24,16},{28,20},{1,9},{5... | collective-permute-start | bytes 12296 | tf_op jit(solution)/shard_map/ppermute | solution.py:25

commit v3 on v2

--- a/solution.py
+++ b/solution.py
@@ -17,7 +17,13 @@
 
 
 def ORDER(n):
-    return sorted(range(1, n), key=lambda k: -k)
+    first = [k for k in [3,2,1] if k < n]
+    return first + [k for k in range(1, n) if k not in first]
+
+
+def FAR(n):
+    first = [k for k in [6,2,4] if k < n]
+    return first + [k for k in range(2, n, 2) if k not in first]
 
 
 def swap(x, axis, k):
@@ -395,28 +401,46 @@
 
 
 def merge_kernel(n, own_ref, recv_ref, *outs):
-    rows = outs[0].shape[0] - 8
+    rows = outs[0].shape[0]
     grp = lax.axis_index("grp")
-    loss = own_ref[n * rows :, :] + recv_ref[n * rows :, :]
-    for k, ref in enumerate(outs):
+    for k, ref in enumerate(outs[:n]):
         at = pl.ds(pl.multiple_of((grp ^ k) * rows, 8), rows)
-        ref[:rows, :] = own_ref[at, :] + recv_ref[at, :]
-        ref[rows:, :] = loss
+        ref[...] = own_ref[at, :] + recv_ref[at, :]
+    outs[n][...] = own_ref[n * rows :, :] + recv_ref[n * rows :, :]
 
 
 def merge(own, recv, n):
-    rows = (own.shape[0] - 8) // n + 8
+    rows = (own.shape[0] - 8) // n
     return pl.pallas_call(
         functools.partial(merge_kernel, n),
-        out_shape=(jax.ShapeDtypeStruct((rows, 128), F32),) * n,
+        out_shape=(jax.ShapeDtypeStruct((rows, 128), F32),) * n
+        + (jax.ShapeDtypeStruct((8, 128), F32),),
         in_specs=specs(2),
-        out_specs=tuple(specs(n)),
+        out_specs=tuple(specs(n + 1)),
         compiler_params=pltpu.CompilerParams(vmem_limit_bytes=16 * MIB),
     )(own, recv)
 
 
-def place_kernel(n, *refs):
-    ranks, out_ref = refs[:n], refs[n]
+def total_kernel(n, *refs):
+    out_ref = refs[-1]
+    rows = refs[0].shape[0]
+    out_ref[:rows, :] = tree_sum([ref[...] for ref in refs[:n]])
+    out_ref[rows:, :] = tree_sum([ref[...] for ref in refs[n:-1]])
+
+
+def total_of(parts, losses):
+    rows = parts[0].shape[0]
+    return pl.pallas_call(
+        functools.partial(total_kernel, len(parts)),
+        out_shape=jax.ShapeDtypeStruct((rows + 8, 128), F32),
+        in_specs=specs(len(parts) + len(losses)),
+        out_specs=specs(1)[0],
+        compiler_params=pltpu.CompilerParams(vmem_limit_bytes=16 * MIB),
+    )(*parts, *losses)
+
+
+def place_kernel(n, count, *refs):
+    ranks, (out_ref, loss_ref) = refs[:n], refs[n:]
     nc, nt, d = out_ref.shape
     lanes = d // 128
     units = nt // 8 * lanes // n
@@ -430,16 +454,20 @@
                 out_ref[c, pl.ds(row, 8), pl.ds(lane, 128)] = ranks[s][
                     pl.ds(8 * nc * i + c, 8, stride=nc), :
                 ]
-
-
-def place(ranks, shape):
-    return pl.pallas_call(
-        functools.partial(place_kernel, len(ranks)),
-        out_shape=jax.ShapeDtypeStruct(shape, F32),
+    loss = tree_sum([ref[ref.shape[0] - 8 :, :] for ref in ranks])
+    loss = jnp.sum(jnp.sum(loss, axis=1, keepdims=True), axis=0, keepdims=True)
+    loss_ref[...] = loss / count
+
+
+def place(ranks, shape, count):
+    text_grads, loss = pl.pallas_call(
+        functools.partial(place_kernel, len(ranks), float(count)),
+        out_shape=(jax.ShapeDtypeStruct(shape, F32), jax.ShapeDtypeStruct((1, 1), F32)),
         in_specs=specs(len(ranks)),
-        out_specs=specs(1)[0],
+        out_specs=tuple(specs(2)),
         compiler_params=pltpu.CompilerParams(vmem_limit_bytes=16 * MIB),
     )(*ranks)
+    return text_grads, loss.reshape(())
 
 
 def steps(image_tokens, text_tokens, labels):
@@ -449,7 +477,7 @@
     count = nb * n_blk * n_grp
     dims = (ni, nb, nt, 2 * nc, d)
     blk = lax.axis_index("blk")
-    far = list(range(2, n_blk, 2))
+    far = FAR(n_blk)
     order = grp_order(n_grp)
 
     mine = pack(jnp.transpose(image_tokens, (1, 0, 2)), labels)
@@ -462,19 +490,20 @@
 
     grads, send, own_part = compute(dims, text_ids, imgs, other, own)
 
-    parts = merge(own_part, swap(send, "blk", 1), n_grp)
+    *parts, loss = merge(own_part, swap(send, "blk", 1), n_grp)
     arrived = {k: swap(parts[k], "grp", k) for k in order}
-    total = tree_sum([parts[0]] + [arrived[k] for k in range(1, n_grp)])
-    rows = total.shape[0] - 8
-    total, loss = total[:rows], total[rows:]
+    losses = [loss] + [swap(loss, "blk", k) for k in sorted(far)]
+    total = total_of(
+        [parts[0]] + [arrived[k] for k in range(1, n_grp)], losses
+    )
     got = {k: swap(total, "grp", k) for k in order}
-    text_grads = place([total] + [got[k] for k in range(1, n_grp)], (nc, nt, d))
+    text_grads, loss = place(
+        [total] + [got[k] for k in range(1, n_grp)], (nc, nt, d), count
+    )
 
     grads = grads[:1] + [swap(g, "blk", k) for k, g in zip(far, grads[1:])]
     image_grads = jnp.transpose(sum_pieces(grads, ni, nb), (1, 0, 2))
 
-    parts = [loss] + [swap(loss, "blk", k) for k in far]
-    loss = jnp.sum(tree_sum(parts)) / count
     return loss, image_grads, text_grads
 
 

time: 54.2 us -> 54.6 us (level)
  starting transfers between devices: 21.6 us -> 24.9 us
  between operations: 2.51 us -> 0.71 us
  other arithmetic: 0.66 us -> 0.02 us
    ppermute x17, starting transfers between devices: 21.6 us -> 24.9 us  [swap(): return lax.ppermute(x, axis, [(i, i ^ k) for i in range(n)])]
    reduce_sum x1 -> x0, other arithmetic: 0.6 us -> none  [steps(): loss = jnp.sum(tree_sum(parts)) / count]
  transfers between devices with their start and end apart: 17 -> 17, of which waited for: 9 -> 9; matrix products, arithmetic and copies ran while one was open for 1% -> 0% of each run, Pallas kernels for 17% -> 18%
where the time goes in v3:
time: 54.6 us; the launch traced here: 54.4 us
  starting transfers between devices  24.9 us (46%)
  waiting for transfers between devices  14.6 us (27%)
  Pallas kernels  14.2 us (26%)
  between operations  0.71 us (1%)
    ppermute x17, starting transfers between devices, swap(): return lax.ppermute(x, axis, [(i, i ^ k) for i in range(n)])  24.9 us
    ppermute x17, waiting for transfers between devices, swap(): return lax.ppermute(x, axis, [(i, i ^ k) for i in range(n)])  14.6 us
    pallas_call x4, Pallas kernels, call(): pl.pallas_call(kernel, out_shape=tuple((jax.ShapeDtypeStruct(*o) for o in...  10 us
    pallas_call x1, Pallas kernels, turn(): pl.pallas_call(functools.partial(turn_kernel, nt), out_shape=jax.ShapeDty...  1.28 us
  transfers between devices with their start and end apart: 17, of which 9 were waited for; matrix products, arithmetic and copies ran while one was open for 0% of the time, Pallas kernels for 18%

profile of v3, /device:TPU:0, one launch (start us, length us, event | category | flops | bytes accessed | tf_op | source)
XLA Modules:
  0.0 54.4 jit_solution(9833049575220026314)
XLA Ops:
  0.6 0.6 %collective-permute-start.3 = (f32[512,256]{1,0:T(8,128)}, f32[512,256]{1,0:T(8,128)S(1)}, u32[]{:S(2)}, u32[]{:S(2)}) collective-permute-start(f32[512,256]{1,0:T(8,128)} %bitcast.5), channel_id=1, source_target_pairs={{0,4},{4,0},{8,12},{12,8},{16,20},{20,16},{24,28},{28,24},{1,5},{5... | collective-permute-start | bytes 1572872 | tf_op jit(solution)/shard_map/ppermute | solution.py:31
  1.2 1.0 %shard_map.58.img_ref = f32[200,256]{1,0:T(8,128)S(1)} custom-call(s32[1,4]{1,0:T(1,128)} %bitcast.9, f32[49,4,256]{2,1,0:T(4,128)} %bitcast.7), custom_call_target="tpu_custom_call" | custom-call | tf_op jit(solution)/shard_map/pallas_call | solution.py:338
  2.2 3.5 %collective-permute-start.2 = (f32[200,256]{1,0:T(8,128)S(1)}, f32[200,256]{1,0:T(8,128)S(1)}, u32[]{:S(2)}, u32[]{:S(2)}) collective-permute-start(f32[200,256]{1,0:T(8,128)S(1)} %shard_map.58.img_ref), channel_id=1, source_target_pairs={{0,24},{4,28},{8,16},{12,20},{16,8},{20,12},{24,0},{28,4},{1,25},{... | collective-permute-start | bytes 614408 | tf_op jit(solution)/shard_map/ppermute | solution.py:31
  5.7 0.5 collective-permute-start.1
  6.4 1.3 %shard_map.59.own_ref = f32[512,256]{1,0:T(8,128)S(1)} custom-call(f32[512,256]{1,0:T(8,128)} %bitcast.6), custom_call_target="tpu_custom_call" | custom-call | tf_op jit(solution)/shard_map/pallas_call | solution.py:373
  7.7 2.9 %shard_map.60 = (f32[200,256]{1,0:T(8,128)S(1)}, f32[256,1024]{1,0:T(8,128)S(1)}, f32[8,128]{1,0:T(8,128)S(1)}, bf16[1024,256]{1,0:T(8,128)(2,1)S(1)}, bf16[1024...) custom-call(s32[8,128]{1,0:T(8,128)S(1)} %fusion.ids_ref, f32[200,256]{1,0:T(8,128)S(1)} %shard_map.58.img_ref, ...), custom_call_target="tpu_custom_call" | custom-call | flops 1233125376 | bytes 1048576 | tf_op jit(solution)/shard_map/pallas_call | solution.py:252
  10.7 1.1 %collective-permute-done.2.refs_0_ = f32[200,256]{1,0:T(8,128)S(1)} collective-permute-done((f32[200,256]{1,0:T(8,128)S(1)}, f32[200,256]{1,0:T(8,128)S(1)}, u32[]{:S(2)}, u32[]{:S(2)}) %collective-permute-start.2) | collective-permute-done | bytes 204832 | tf_op jit(solution)/shard_map/ppermute | solution.py:31
  11.7 2.6 %shard_map.61 = (f32[200,256]{1,0:T(8,128)S(1)}, f32[256,1024]{1,0:T(8,128)S(1)}, f32[8,128]{1,0:T(8,128)S(1)}) custom-call(s32[8,128]{1,0:T(8,128)S(1)} %fusion.ids_ref, f32[200,256]{1,0:T(8,128)S(1)} %collective-permute-done.2.refs_0_, f32[256,1024]{1,0:T(8,128)S(1)} %get-tuple-element.27.refs_1_, f32[8,128]{1,0:T(8,128)S(1)} %get-tuple-element.28.refs_2_, ...), custom_call_target="tpu_custom_call" | custom-call | flops 1233125376 | bytes 1048576 | tf_op jit(solution)/shard_map/pallas_call | solution.py:252
  14.3 1.6 %collective-permute-done.1.refs_1_ = f32[200,256]{1,0:T(8,128)S(1)} collective-permute-done((f32[200,256]{1,0:T(8,128)S(1)}, f32[200,256]{1,0:T(8,128)S(1)}, u32[]{:S(2)}, u32[]{:S(2)}) %collective-permute-start.1) | collective-permute-done | bytes 204832 | tf_op jit(solution)/shard_map/ppermute | solution.py:31
  15.9 0.3 collective-permute-done.refs_0_
  16.2 3.7 %shard_map.62 = (f32[1032,128]{1,0:T(8,128)S(1)}, f32[1032,128]{1,0:T(8,128)S(1)}, bf16[200,1024]{1,0:T(8,128)(2,1)S(1)}, bf16[200,1024]{1,0:T(8,128)(2,1)S(1)},...) custom-call(s32[8,128]{1,0:T(8,128)S(1)} %fusion.ids_ref, f32[200,256]{1,0:T(8,128)S(1)} %collective-permute-done.refs_0_, ...), custom_call_target="tpu_custom_call" | custom-call | flops 1849688064 | bytes 1048576 | tf_op jit(solution)/shard_map/pallas_call | solution.py:252
  19.9 1.6 %collective-permute-start.14 = (f32[200,256]{1,0:T(8,128)S(1)}, f32[200,256]{1,0:T(8,128)S(1)}, u32[]{:S(2)}, u32[]{:S(2)}) collective-permute-start(f32[200,256]{1,0:T(8,128)S(1)} %get-tuple-element.43), channel_id=1, source_target_pairs={{0,24},{4,28},{8,16},{12,20},{16,8},{20,12},{24,0},{28,4},{1,25},{... | collective-permute-start | bytes 614408 | tf_op jit(solution)/shard_map/ppermute | solution.py:31
  21.5 0.3 collective-permute-done.4.recv_ref
  21.9 1.6 %collective-permute-start.5 = (f32[256,128]{1,0:T(8,128)S(1)}, f32[256,128]{1,0:T(8,128)S(1)}, u32[]{:S(2)}, u32[]{:S(2)}) collective-permute-start(f32[256,128]{1,0:T(8,128)S(1)} %get-tuple-element.37), channel_id=1, source_target_pairs={{0,1},{1,0},{2,3},{3,2},{4,5},{5,4},{6,7},{7,6},{8,9},{9,8},{10,11... | collective-permute-start | bytes 393224 | tf_op jit(solution)/shard_map/ppermute | solution.py:31
  23.6 1.7 %collective-permute-start.10 = (f32[8,128]{1,0:T(8,128)S(1)}, f32[8,128]{1,0:T(8,128)S(1)}, u32[]{:S(2)}, u32[]{:S(2)}) collective-permute-start(f32[8,128]{1,0:T(8,128)S(1)} %get-tuple-element.40.refs_4_), channel_id=1, source_target_pairs={{0,24},{4,28},{8,16},{12,20},{16,8},{20,12},{24,0},{28,4},{1,25},{... | collective-permute-start | bytes 12296 | tf_op jit(solution)/shard_map/ppermute | solution.py:31
  25.2 1.3 %collective-permute-start.9 = (f32[8,128]{1,0:T(8,128)S(1)}, f32[8,128]{1,0:T(8,128)S(1)}, u32[]{:S(2)}, u32[]{:S(2)}) collective-permute-start(f32[8,128]{1,0:T(8,128)S(1)} %get-tuple-element.40.refs_4_), channel_id=1, source_target_pairs={{0,16},{4,20},{8,24},{12,28},{16,0},{20,4},{24,8},{28,12},{1,17},{... | collective-permute-start | bytes 12296 | tf_op jit(solution)/shard_map/ppermute | solution.py:31
  26.5 2.6 %collective-permute-start.6 = (f32[256,128]{1,0:T(8,128)S(1)}, f32[256,128]{1,0:T(8,128)S(1)}, u32[]{:S(2)}, u32[]{:S(2)}) collective-permute-start(f32[256,128]{1,0:T(8,128)S(1)} %get-tuple-element.38), channel_id=1, source_target_pairs={{0,2},{1,3},{2,0},{3,1},{4,6},{5,7},{6,4},{7,5},{8,10},{9,11},{10,... | collective-permute-start | bytes 393224 | tf_op jit(solution)/shard_map/ppermute | solution.py:31
  29.1 3.0 %collective-permute-start.7 = (f32[256,128]{1,0:T(8,128)S(1)}, f32[256,128]{1,0:T(8,128)S(1)}, u32[]{:S(2)}, u32[]{:S(2)}) collective-permute-start(f32[256,128]{1,0:T(8,128)S(1)} %get-tuple-element.39), channel_id=1, source_target_pairs={{0,3},{1,2},{2,1},{3,0},{4,7},{5,6},{6,5},{7,4},{8,11},{9,10},{10,... | collective-permute-start | bytes 393224 | tf_op jit(solution)/shard_map/ppermute | solution.py:31
  32.1 1.5 %collective-permute-start.8 = (f32[8,128]{1,0:T(8,128)S(1)}, f32[8,128]{1,0:T(8,128)S(1)}, u32[]{:S(2)}, u32[]{:S(2)}) collective-permute-start(f32[8,128]{1,0:T(8,128)S(1)} %get-tuple-element.40.refs_4_), channel_id=1, source_target_pairs={{0,8},{4,12},{8,0},{12,4},{16,24},{20,28},{24,16},{28,20},{1,9},{5... | collective-permute-start | bytes 12296 | tf_op jit(solution)/shard_map/ppermute | solution.py:31
  33.6 0.8 %shard_map.66 = (f32[200,256]{1,0:T(8,128)S(1)}, f32[200,256]{1,0:T(8,128)S(1)}) custom-call(bf16[1024,256]{1,0:T(8,128)(2,1)S(1)} %get-tuple-element.29.refs_3_.refs_4_.th_ref, bf16[1024,256]{1,0:T(8,128)(2,1)S(1)} %get-tuple-element.30.refs_4_.refs_5_.tm_ref, bf16[200,1024]{1,0:T(8,128)(2,1)S(1)} %get-tuple-element.44.refs_0_, ...), custom_call_target="tpu_custom_call" | custom-call | flops 616562688 | bytes 1048576 | tf_op jit(solution)/shard_map/pallas_call | solution.py:252
  34.4 1.3 %collective-permute-done.8.refs_5_ = f32[8,128]{1,0:T(8,128)S(1)} collective-permute-done((f32[8,128]{1,0:T(8,128)S(1)}, f32[8,128]{1,0:T(8,128)S(1)}, u32[]{:S(2)}, u32[]{:S(2)}) %collective-permute-start.8) | collective-permute-done | bytes 4128 | tf_op jit(solution)/shard_map/ppermute | solution.py:31
  35.7 1.5 %collective-permute-start.15 = (f32[200,256]{1,0:T(8,128)S(1)}, f32[200,256]{1,0:T(8,128)S(1)}, u32[]{:S(2)}, u32[]{:S(2)}) collective-permute-start(f32[200,256]{1,0:T(8,128)S(1)} %get-tuple-element.48), channel_id=1, source_target_pairs={{0,8},{4,12},{8,0},{12,4},{16,24},{20,28},{24,16},{28,20},{1,9},{5... | collective-permute-start | bytes 614408 | tf_op jit(solution)/shard_map/ppermute | solution.py:31
  37.2 0.7 %collective-permute-start.16 = (f32[200,256]{1,0:T(8,128)S(1)}, f32[200,256]{1,0:T(8,128)S(1)}, u32[]{:S(2)}, u32[]{:S(2)}) collective-permute-start(f32[200,256]{1,0:T(8,128)S(1)} %get-tuple-element.49), channel_id=1, source_target_pairs={{0,16},{4,20},{8,24},{12,28},{16,0},{20,4},{24,8},{28,12},{1,17},{... | collective-permute-start | bytes 614408 | tf_op jit(solution)/shard_map/ppermute | solution.py:31
  37.9 0.1 collective-permute-done.6.refs_2_
  38.1 3.3 %collective-permute-start.13 = (f32[264,128]{1,0:T(8,128)S(1)}, f32[264,128]{1,0:T(8,128)S(1)}, u32[]{:S(2)}, u32[]{:S(2)}) collective-permute-start(f32[264,128]{1,0:T(8,128)S(1)} %shard_map.64.refs_0_), channel_id=1, source_target_pairs={{0,3},{1,2},{2,1},{3,0},{4,7},{5,6},{6,5},{7,4},{8,11},{9,10},{10,... | collective-permute-start | bytes 405512 | tf_op jit(solution)/shard_map/ppermute | solution.py:31
  41.4 1.2 %collective-permute-start.12 = (f32[264,128]{1,0:T(8,128)S(1)}, f32[264,128]{1,0:T(8,128)S(1)}, u32[]{:S(2)}, u32[]{:S(2)}) collective-permute-start(f32[264,128]{1,0:T(8,128)S(1)} %shard_map.64.refs_0_), channel_id=1, source_target_pairs={{0,2},{1,3},{2,0},{3,1},{4,6},{5,7},{6,4},{7,5},{8,10},{9,11},{10,... | collective-permute-start | bytes 405512 | tf_op jit(solution)/shard_map/ppermute | solution.py:31
  42.6 0.2 collective-permute-start.11
  42.8 0.2 collective-permute-done.16.refs_3_
  42.9 0.8 %shard_map.67 = f32[49,4,256]{2,1,0:T(4,128)} custom-call(f32[200,256]{1,0:T(8,128)S(1)} %get-tuple-element.42.refs_0_, f32[200,256]{1,0:T(8,128)S(1)} %collective-permute-done.14.refs_1_, f32[200,256]{1,0:T(8,128)S(1)} %collective-permute-done.15.refs_2_, f32[200,256]{1,0:T(8,128)S(1)} %collective-permute-done.16.refs_3_), custom_call_target="tpu_custom_call" | custom-call | tf_op jit(solution)/shard_map/pallas_call | solution.py:394
  43.7 1.8 %collective-permute-done.13.refs_3_ = f32[264,128]{1,0:T(8,128)S(1)} collective-permute-done((f32[264,128]{1,0:T(8,128)S(1)}, f32[264,128]{1,0:T(8,128)S(1)}, u32[]{:S(2)}, u32[]{:S(2)}) %collective-permute-start.13) | collective-permute-done | bytes 135200 | tf_op jit(solution)/shard_map/ppermute | solution.py:31
  45.5 7.9 %collective-permute-done.12.refs_2_ = f32[264,128]{1,0:T(8,128)S(1)} collective-permute-done((f32[264,128]{1,0:T(8,128)S(1)}, f32[264,128]{1,0:T(8,128)S(1)}, u32[]{:S(2)}, u32[]{:S(2)}) %collective-permute-start.12) | collective-permute-done | bytes 135200 | tf_op jit(solution)/shard_map/ppermute | solution.py:31
  53.5 1.0 %shard_map.65 = (f32[16,32,256]{2,1,0:T(8,128)}, f32[1,1]{1,0:T(1,128)}) custom-call(f32[264,128]{1,0:T(8,128)S(1)} %shard_map.64.refs_0_, f32[264,128]{1,0:T(8,128)S(1)} %collective-permute-done.11.refs_1_, f32[264,128]{1,0:T(8,128)S(1)} %collective-permute-done.12.refs_2_, f32[264,128]{1,0:T(8,128)S(1)} %collective-permute-done.13.refs_3_), custom_call_target="tpu_custom_call" | custom-call | tf_op jit(solution)/shard_map/pallas_call | solution.py:463
  (15 shorter events, 0.4 us)
Async XLA Ops:
  0.6 7.1 %collective-permute-start.3 = (f32[512,256]{1,0:T(8,128)}, f32[512,256]{1,0:T(8,128)S(1)}, u32[]{:S(2)}, u32[]{:S(2)}) collective-permute-start(f32[512,256]{1,0:T(8,128)} %bitcast.5), channel_id=1, source_target_pairs={{0,4},{4,0},{8,12},{12,8},{16,20},{20,16},{24,28},{28,24},{1,5},{5... | collective-permute-start | bytes 1572872 | tf_op jit(solution)/shard_map/ppermute | solution.py:31
  2.2 9.5 %collective-permute-start.2 = (f32[200,256]{1,0:T(8,128)S(1)}, f32[200,256]{1,0:T(8,128)S(1)}, u32[]{:S(2)}, u32[]{:S(2)}) collective-permute-start(f32[200,256]{1,0:T(8,128)S(1)} %shard_map.58.img_ref), channel_id=1, source_target_pairs={{0,24},{4,28},{8,16},{12,20},{16,8},{20,12},{24,0},{28,4},{1,25},{... | collective-permute-start | bytes 614408 | tf_op jit(solution)/shard_map/ppermute | solution.py:31
  5.7 10.1 %collective-permute-start.1 = (f32[200,256]{1,0:T(8,128)S(1)}, f32[200,256]{1,0:T(8,128)S(1)}, u32[]{:S(2)}, u32[]{:S(2)}) collective-permute-start(f32[200,256]{1,0:T(8,128)S(1)} %shard_map.58.img_ref), channel_id=1, source_target_pairs={{0,16},{4,20},{8,24},{12,28},{16,0},{20,4},{24,8},{28,12},{1,17},{... | collective-permute-start | bytes 614408 | tf_op jit(solution)/shard_map/ppermute | solution.py:31
  6.3 9.9 %collective-permute-start = (f32[200,256]{1,0:T(8,128)S(1)}, f32[200,256]{1,0:T(8,128)S(1)}, u32[]{:S(2)}, u32[]{:S(2)}) collective-permute-start(f32[200,256]{1,0:T(8,128)S(1)} %shard_map.58.img_ref), channel_id=1, source_target_pairs={{0,8},{4,12},{8,0},{12,4},{16,24},{20,28},{24,16},{28,20},{1,9},{5... | collective-permute-start | bytes 614408 | tf_op jit(solution)/shard_map/ppermute | solution.py:31
  19.8 2.0 %collective-permute-start.4 = (f32[1032,128]{1,0:T(8,128)S(1)}, f32[1032,128]{1,0:T(8,128)S(1)}, u32[]{:S(2)}, u32[]{:S(2)}) collective-permute-start(f32[1032,128]{1,0:T(8,128)S(1)} %get-tuple-element.35), channel_id=1, source_target_pairs={{0,4},{4,0},{8,12},{12,8},{16,20},{20,16},{24,28},{28,24},{1,5},{5... | collective-permute-start | bytes 1585160 | tf_op jit(solution)/shard_map/ppermute | solution.py:31
  19.9 22.7 %collective-permute-start.14 = (f32[200,256]{1,0:T(8,128)S(1)}, f32[200,256]{1,0:T(8,128)S(1)}, u32[]{:S(2)}, u32[]{:S(2)}) collective-permute-start(f32[200,256]{1,0:T(8,128)S(1)} %get-tuple-element.43), channel_id=1, source_target_pairs={{0,24},{4,28},{8,16},{12,20},{16,8},{20,12},{24,0},{28,4},{1,25},{... | collective-permute-start | bytes 614408 | tf_op jit(solution)/shard_map/ppermute | solution.py:31
  21.9 15.3 %collective-permute-start.5 = (f32[256,128]{1,0:T(8,128)S(1)}, f32[256,128]{1,0:T(8,128)S(1)}, u32[]{:S(2)}, u32[]{:S(2)}) collective-permute-start(f32[256,128]{1,0:T(8,128)S(1)} %get-tuple-element.37), channel_id=1, source_target_pairs={{0,1},{1,0},{2,3},{3,2},{4,5},{5,4},{6,7},{7,6},{8,9},{9,8},{10,11... | collective-permute-start | bytes 393224 | tf_op jit(solution)/shard_map/ppermute | solution.py:31
  23.6 5.5 %collective-permute-start.10 = (f32[8,128]{1,0:T(8,128)S(1)}, f32[8,128]{1,0:T(8,128)S(1)}, u32[]{:S(2)}, u32[]{:S(2)}) collective-permute-start(f32[8,128]{1,0:T(8,128)S(1)} %get-tuple-element.40.refs_4_), channel_id=1, source_target_pairs={{0,24},{4,28},{8,16},{12,20},{16,8},{20,12},{24,0},{28,4},{1,25},{... | collective-permute-start | bytes 12296 | tf_op jit(solution)/shard_map/ppermute | solution.py:31
  25.2 6.9 %collective-permute-start.9 = (f32[8,128]{1,0:T(8,128)S(1)}, f32[8,128]{1,0:T(8,128)S(1)}, u32[]{:S(2)}, u32[]{:S(2)}) collective-permute-start(f32[8,128]{1,0:T(8,128)S(1)} %get-tuple-element.40.refs_4_), channel_id=1, source_target_pairs={{0,16},{4,20},{8,24},{12,28},{16,0},{20,4},{24,8},{28,12},{1,17},{... | collective-permute-start | bytes 12296 | tf_op jit(solution)/shard_map/ppermute | solution.py:31
  26.5 11.5 %collective-permute-start.6 = (f32[256,128]{1,0:T(8,128)S(1)}, f32[256,128]{1,0:T(8,128)S(1)}, u32[]{:S(2)}, u32[]{:S(2)}) collective-permute-start(f32[256,128]{1,0:T(8,128)S(1)} %get-tuple-element.38), channel_id=1, source_target_pairs={{0,2},{1,3},{2,0},{3,1},{4,6},{5,7},{6,4},{7,5},{8,10},{9,11},{10,... | collective-permute-start | bytes 393224 | tf_op jit(solution)/shard_map/ppermute | solution.py:31
  29.1 9.0 %collective-permute-start.7 = (f32[256,128]{1,0:T(8,128)S(1)}, f32[256,128]{1,0:T(8,128)S(1)}, u32[]{:S(2)}, u32[]{:S(2)}) collective-permute-start(f32[256,128]{1,0:T(8,128)S(1)} %get-tuple-element.39), channel_id=1, source_target_pairs={{0,3},{1,2},{2,1},{3,0},{4,7},{5,6},{6,5},{7,4},{8,11},{9,10},{10,... | collective-permute-start | bytes 393224 | tf_op jit(solution)/shard_map/ppermute | solution.py:31
  32.1 3.6 %collective-permute-start.8 = (f32[8,128]{1,0:T(8,128)S(1)}, f32[8,128]{1,0:T(8,128)S(1)}, u32[]{:S(2)}, u32[]{:S(2)}) collective-permute-start(f32[8,128]{1,0:T(8,128)S(1)} %get-tuple-element.40.refs_4_), channel_id=1, source_target_pairs={{0,8},{4,12},{8,0},{12,4},{16,24},{20,28},{24,16},{28,20},{1,9},{5... | collective-permute-start | bytes 12296 | tf_op jit(solution)/shard_map/ppermute | solution.py:31
  35.7 7.1 %collective-permute-start.15 = (f32[200,256]{1,0:T(8,128)S(1)}, f32[200,256]{1,0:T(8,128)S(1)}, u32[]{:S(2)}, u32[]{:S(2)}) collective-permute-start(f32[200,256]{1,0:T(8,128)S(1)} %get-tuple-element.48), channel_id=1, source_target_pairs={{0,8},{4,12},{8,0},{12,4},{16,24},{20,28},{24,16},{28,20},{1,9},{5... | collective-permute-start | bytes 614408 | tf_op jit(solution)/shard_map/ppermute | solution.py:31
  37.2 5.8 %collective-permute-start.16 = (f32[200,256]{1,0:T(8,128)S(1)}, f32[200,256]{1,0:T(8,128)S(1)}, u32[]{:S(2)}, u32[]{:S(2)}) collective-permute-start(f32[200,256]{1,0:T(8,128)S(1)} %get-tuple-element.49), channel_id=1, source_target_pairs={{0,16},{4,20},{8,24},{12,28},{16,0},{20,4},{24,8},{28,12},{1,17},{... | collective-permute-start | bytes 614408 | tf_op jit(solution)/shard_map/ppermute | solution.py:31
  38.1 7.4 %collective-permute-start.13 = (f32[264,128]{1,0:T(8,128)S(1)}, f32[264,128]{1,0:T(8,128)S(1)}, u32[]{:S(2)}, u32[]{:S(2)}) collective-permute-start(f32[264,128]{1,0:T(8,128)S(1)} %shard_map.64.refs_0_), channel_id=1, source_target_pairs={{0,3},{1,2},{2,1},{3,0},{4,7},{5,6},{6,5},{7,4},{8,11},{9,10},{10,... | collective-permute-start | bytes 405512 | tf_op jit(solution)/shard_map/ppermute | solution.py:31
  41.4 12.1 %collective-permute-start.12 = (f32[264,128]{1,0:T(8,128)S(1)}, f32[264,128]{1,0:T(8,128)S(1)}, u32[]{:S(2)}, u32[]{:S(2)}) collective-permute-start(f32[264,128]{1,0:T(8,128)S(1)} %shard_map.64.refs_0_), channel_id=1, source_target_pairs={{0,2},{1,3},{2,0},{3,1},{4,6},{5,7},{6,4},{7,5},{8,10},{9,11},{10,... | collective-permute-start | bytes 405512 | tf_op jit(solution)/shard_map/ppermute | solution.py:31
  42.6 10.9 %collective-permute-start.11 = (f32[264,128]{1,0:T(8,128)S(1)}, f32[264,128]{1,0:T(8,128)S(1)}, u32[]{:S(2)}, u32[]{:S(2)}) collective-permute-start(f32[264,128]{1,0:T(8,128)S(1)} %shard_map.64.refs_0_), channel_id=1, source_target_pairs={{0,1},{1,0},{2,3},{3,2},{4,5},{5,4},{6,7},{7,6},{8,9},{9,8},{10,11... | collective-permute-start | bytes 405512 | tf_op jit(solution)/shard_map/ppermute | solution.py:31

commit v4 on v3

--- a/solution.py
+++ b/solution.py
@@ -14,11 +14,6 @@
 LOG2E = 1.4426950408889634
 LN2 = 0.6931471805599453
 MIB = 1024 * 1024
-
-
-def ORDER(n):
-    first = [k for k in [3,2,1] if k < n]
-    return first + [k for k in range(1, n) if k not in first]
 
 
 def FAR(n):
@@ -508,7 +503,7 @@
 
 
 def grp_order(n_grp):
-    return ORDER(n_grp)
+    return list(range(n_grp - 1, 0, -1))
 
 
 def solution(mesh):

time: 54.6 us -> 54.6 us (level)
  no operation moved by 1% of the time
where the time goes in v4:
time: 54.6 us; the launch traced here: 54.4 us
  starting transfers between devices  24.9 us (46%)
  waiting for transfers between devices  14.6 us (27%)
  Pallas kernels  14.2 us (26%)
  between operations  0.71 us (1%)
    ppermute x17, starting transfers between devices, swap(): return lax.ppermute(x, axis, [(i, i ^ k) for i in range(n)])  24.9 us
    ppermute x17, waiting for transfers between devices, swap(): return lax.ppermute(x, axis, [(i, i ^ k) for i in range(n)])  14.6 us
    pallas_call x4, Pallas kernels, call(): pl.pallas_call(kernel, out_shape=tuple((jax.ShapeDtypeStruct(*o) for o in...  10 us
    pallas_call x1, Pallas kernels, turn(): pl.pallas_call(functools.partial(turn_kernel, nt), out_shape=jax.ShapeDty...  1.28 us
  transfers between devices with their start and end apart: 17, of which 9 were waited for; matrix products, arithmetic and copies ran while one was open for 0% of the time, Pallas kernels for 18%

profile of v4, /device:TPU:0, one launch (start us, length us, event | category | flops | bytes accessed | tf_op | source)
XLA Modules:
  0.0 54.4 jit_solution(9833049575220026314)
XLA Ops:
  0.6 0.6 %collective-permute-start.3 = (f32[512,256]{1,0:T(8,128)}, f32[512,256]{1,0:T(8,128)S(1)}, u32[]{:S(2)}, u32[]{:S(2)}) collective-permute-start(f32[512,256]{1,0:T(8,128)} %bitcast.5), channel_id=1, source_target_pairs={{0,4},{4,0},{8,12},{12,8},{16,20},{20,16},{24,28},{28,24},{1,5},{5... | collective-permute-start | bytes 1572872 | tf_op jit(solution)/shard_map/ppermute | solution.py:26
  1.2 1.0 %shard_map.58.img_ref = f32[200,256]{1,0:T(8,128)S(1)} custom-call(s32[1,4]{1,0:T(1,128)} %bitcast.9, f32[49,4,256]{2,1,0:T(4,128)} %bitcast.7), custom_call_target="tpu_custom_call" | custom-call | tf_op jit(solution)/shard_map/pallas_call | solution.py:333
  2.2 3.5 %collective-permute-start.2 = (f32[200,256]{1,0:T(8,128)S(1)}, f32[200,256]{1,0:T(8,128)S(1)}, u32[]{:S(2)}, u32[]{:S(2)}) collective-permute-start(f32[200,256]{1,0:T(8,128)S(1)} %shard_map.58.img_ref), channel_id=1, source_target_pairs={{0,24},{4,28},{8,16},{12,20},{16,8},{20,12},{24,0},{28,4},{1,25},{... | collective-permute-start | bytes 614408 | tf_op jit(solution)/shard_map/ppermute | solution.py:26
  5.7 0.5 collective-permute-start.1
  6.4 1.3 %shard_map.59.own_ref = f32[512,256]{1,0:T(8,128)S(1)} custom-call(f32[512,256]{1,0:T(8,128)} %bitcast.6), custom_call_target="tpu_custom_call" | custom-call | tf_op jit(solution)/shard_map/pallas_call | solution.py:368
  7.7 2.9 %shard_map.60 = (f32[200,256]{1,0:T(8,128)S(1)}, f32[256,1024]{1,0:T(8,128)S(1)}, f32[8,128]{1,0:T(8,128)S(1)}, bf16[1024,256]{1,0:T(8,128)(2,1)S(1)}, bf16[1024...) custom-call(s32[8,128]{1,0:T(8,128)S(1)} %fusion.ids_ref, f32[200,256]{1,0:T(8,128)S(1)} %shard_map.58.img_ref, ...), custom_call_target="tpu_custom_call" | custom-call | flops 1233125376 | bytes 1048576 | tf_op jit(solution)/shard_map/pallas_call | solution.py:247
  10.7 1.1 %collective-permute-done.2.refs_0_ = f32[200,256]{1,0:T(8,128)S(1)} collective-permute-done((f32[200,256]{1,0:T(8,128)S(1)}, f32[200,256]{1,0:T(8,128)S(1)}, u32[]{:S(2)}, u32[]{:S(2)}) %collective-permute-start.2) | collective-permute-done | bytes 204832 | tf_op jit(solution)/shard_map/ppermute | solution.py:26
  11.7 2.6 %shard_map.61 = (f32[200,256]{1,0:T(8,128)S(1)}, f32[256,1024]{1,0:T(8,128)S(1)}, f32[8,128]{1,0:T(8,128)S(1)}) custom-call(s32[8,128]{1,0:T(8,128)S(1)} %fusion.ids_ref, f32[200,256]{1,0:T(8,128)S(1)} %collective-permute-done.2.refs_0_, f32[256,1024]{1,0:T(8,128)S(1)} %get-tuple-element.27.refs_1_, f32[8,128]{1,0:T(8,128)S(1)} %get-tuple-element.28.refs_2_, ...), custom_call_target="tpu_custom_call" | custom-call | flops 1233125376 | bytes 1048576 | tf_op jit(solution)/shard_map/pallas_call | solution.py:247
  14.3 1.6 %collective-permute-done.1.refs_1_ = f32[200,256]{1,0:T(8,128)S(1)} collective-permute-done((f32[200,256]{1,0:T(8,128)S(1)}, f32[200,256]{1,0:T(8,128)S(1)}, u32[]{:S(2)}, u32[]{:S(2)}) %collective-permute-start.1) | collective-permute-done | bytes 204832 | tf_op jit(solution)/shard_map/ppermute | solution.py:26
  15.9 0.3 collective-permute-done.refs_0_
  16.2 3.7 %shard_map.62 = (f32[1032,128]{1,0:T(8,128)S(1)}, f32[1032,128]{1,0:T(8,128)S(1)}, bf16[200,1024]{1,0:T(8,128)(2,1)S(1)}, bf16[200,1024]{1,0:T(8,128)(2,1)S(1)},...) custom-call(s32[8,128]{1,0:T(8,128)S(1)} %fusion.ids_ref, f32[200,256]{1,0:T(8,128)S(1)} %collective-permute-done.refs_0_, ...), custom_call_target="tpu_custom_call" | custom-call | flops 1849688064 | bytes 1048576 | tf_op jit(solution)/shard_map/pallas_call | solution.py:247
  19.9 1.6 %collective-permute-start.14 = (f32[200,256]{1,0:T(8,128)S(1)}, f32[200,256]{1,0:T(8,128)S(1)}, u32[]{:S(2)}, u32[]{:S(2)}) collective-permute-start(f32[200,256]{1,0:T(8,128)S(1)} %get-tuple-element.43), channel_id=1, source_target_pairs={{0,24},{4,28},{8,16},{12,20},{16,8},{20,12},{24,0},{28,4},{1,25},{... | collective-permute-start | bytes 614408 | tf_op jit(solution)/shard_map/ppermute | solution.py:26
  21.5 0.3 collective-permute-done.4.recv_ref
  21.9 1.6 %collective-permute-start.5 = (f32[256,128]{1,0:T(8,128)S(1)}, f32[256,128]{1,0:T(8,128)S(1)}, u32[]{:S(2)}, u32[]{:S(2)}) collective-permute-start(f32[256,128]{1,0:T(8,128)S(1)} %get-tuple-element.37), channel_id=1, source_target_pairs={{0,1},{1,0},{2,3},{3,2},{4,5},{5,4},{6,7},{7,6},{8,9},{9,8},{10,11... | collective-permute-start | bytes 393224 | tf_op jit(solution)/shard_map/ppermute | solution.py:26
  23.6 1.7 %collective-permute-start.10 = (f32[8,128]{1,0:T(8,128)S(1)}, f32[8,128]{1,0:T(8,128)S(1)}, u32[]{:S(2)}, u32[]{:S(2)}) collective-permute-start(f32[8,128]{1,0:T(8,128)S(1)} %get-tuple-element.40.refs_4_), channel_id=1, source_target_pairs={{0,24},{4,28},{8,16},{12,20},{16,8},{20,12},{24,0},{28,4},{1,25},{... | collective-permute-start | bytes 12296 | tf_op jit(solution)/shard_map/ppermute | solution.py:26
  25.2 1.3 %collective-permute-start.9 = (f32[8,128]{1,0:T(8,128)S(1)}, f32[8,128]{1,0:T(8,128)S(1)}, u32[]{:S(2)}, u32[]{:S(2)}) collective-permute-start(f32[8,128]{1,0:T(8,128)S(1)} %get-tuple-element.40.refs_4_), channel_id=1, source_target_pairs={{0,16},{4,20},{8,24},{12,28},{16,0},{20,4},{24,8},{28,12},{1,17},{... | collective-permute-start | bytes 12296 | tf_op jit(solution)/shard_map/ppermute | solution.py:26
  26.5 2.6 %collective-permute-start.6 = (f32[256,128]{1,0:T(8,128)S(1)}, f32[256,128]{1,0:T(8,128)S(1)}, u32[]{:S(2)}, u32[]{:S(2)}) collective-permute-start(f32[256,128]{1,0:T(8,128)S(1)} %get-tuple-element.38), channel_id=1, source_target_pairs={{0,2},{1,3},{2,0},{3,1},{4,6},{5,7},{6,4},{7,5},{8,10},{9,11},{10,... | collective-permute-start | bytes 393224 | tf_op jit(solution)/shard_map/ppermute | solution.py:26
  29.1 3.0 %collective-permute-start.7 = (f32[256,128]{1,0:T(8,128)S(1)}, f32[256,128]{1,0:T(8,128)S(1)}, u32[]{:S(2)}, u32[]{:S(2)}) collective-permute-start(f32[256,128]{1,0:T(8,128)S(1)} %get-tuple-element.39), channel_id=1, source_target_pairs={{0,3},{1,2},{2,1},{3,0},{4,7},{5,6},{6,5},{7,4},{8,11},{9,10},{10,... | collective-permute-start | bytes 393224 | tf_op jit(solution)/shard_map/ppermute | solution.py:26
  32.1 1.5 %collective-permute-start.8 = (f32[8,128]{1,0:T(8,128)S(1)}, f32[8,128]{1,0:T(8,128)S(1)}, u32[]{:S(2)}, u32[]{:S(2)}) collective-permute-start(f32[8,128]{1,0:T(8,128)S(1)} %get-tuple-element.40.refs_4_), channel_id=1, source_target_pairs={{0,8},{4,12},{8,0},{12,4},{16,24},{20,28},{24,16},{28,20},{1,9},{5... | collective-permute-start | bytes 12296 | tf_op jit(solution)/shard_map/ppermute | solution.py:26
  33.6 0.8 %shard_map.66 = (f32[200,256]{1,0:T(8,128)S(1)}, f32[200,256]{1,0:T(8,128)S(1)}) custom-call(bf16[1024,256]{1,0:T(8,128)(2,1)S(1)} %get-tuple-element.29.refs_3_.refs_4_.th_ref, bf16[1024,256]{1,0:T(8,128)(2,1)S(1)} %get-tuple-element.30.refs_4_.refs_5_.tm_ref, bf16[200,1024]{1,0:T(8,128)(2,1)S(1)} %get-tuple-element.44.refs_0_, ...), custom_call_target="tpu_custom_call" | custom-call | flops 616562688 | bytes 1048576 | tf_op jit(solution)/shard_map/pallas_call | solution.py:247
  34.4 1.3 %collective-permute-done.8.refs_5_ = f32[8,128]{1,0:T(8,128)S(1)} collective-permute-done((f32[8,128]{1,0:T(8,128)S(1)}, f32[8,128]{1,0:T(8,128)S(1)}, u32[]{:S(2)}, u32[]{:S(2)}) %collective-permute-start.8) | collective-permute-done | bytes 4128 | tf_op jit(solution)/shard_map/ppermute | solution.py:26
  35.7 1.5 %collective-permute-start.15 = (f32[200,256]{1,0:T(8,128)S(1)}, f32[200,256]{1,0:T(8,128)S(1)}, u32[]{:S(2)}, u32[]{:S(2)}) collective-permute-start(f32[200,256]{1,0:T(8,128)S(1)} %get-tuple-element.48), channel_id=1, source_target_pairs={{0,8},{4,12},{8,0},{12,4},{16,24},{20,28},{24,16},{28,20},{1,9},{5... | collective-permute-start | bytes 614408 | tf_op jit(solution)/shard_map/ppermute | solution.py:26
  37.2 0.7 %collective-permute-start.16 = (f32[200,256]{1,0:T(8,128)S(1)}, f32[200,256]{1,0:T(8,128)S(1)}, u32[]{:S(2)}, u32[]{:S(2)}) collective-permute-start(f32[200,256]{1,0:T(8,128)S(1)} %get-tuple-element.49), channel_id=1, source_target_pairs={{0,16},{4,20},{8,24},{12,28},{16,0},{20,4},{24,8},{28,12},{1,17},{... | collective-permute-start | bytes 614408 | tf_op jit(solution)/shard_map/ppermute | solution.py:26
  37.9 0.1 collective-permute-done.6.refs_2_
  38.1 3.3 %collective-permute-start.13 = (f32[264,128]{1,0:T(8,128)S(1)}, f32[264,128]{1,0:T(8,128)S(1)}, u32[]{:S(2)}, u32[]{:S(2)}) collective-permute-start(f32[264,128]{1,0:T(8,128)S(1)} %shard_map.64.refs_0_), channel_id=1, source_target_pairs={{0,3},{1,2},{2,1},{3,0},{4,7},{5,6},{6,5},{7,4},{8,11},{9,10},{10,... | collective-permute-start | bytes 405512 | tf_op jit(solution)/shard_map/ppermute | solution.py:26
  41.4 1.2 %collective-permute-start.12 = (f32[264,128]{1,0:T(8,128)S(1)}, f32[264,128]{1,0:T(8,128)S(1)}, u32[]{:S(2)}, u32[]{:S(2)}) collective-permute-start(f32[264,128]{1,0:T(8,128)S(1)} %shard_map.64.refs_0_), channel_id=1, source_target_pairs={{0,2},{1,3},{2,0},{3,1},{4,6},{5,7},{6,4},{7,5},{8,10},{9,11},{10,... | collective-permute-start | bytes 405512 | tf_op jit(solution)/shard_map/ppermute | solution.py:26
  42.6 0.2 collective-permute-start.11
  42.8 0.2 collective-permute-done.16.refs_3_
  42.9 0.8 %shard_map.67 = f32[49,4,256]{2,1,0:T(4,128)} custom-call(f32[200,256]{1,0:T(8,128)S(1)} %get-tuple-element.42.refs_0_, f32[200,256]{1,0:T(8,128)S(1)} %collective-permute-done.14.refs_1_, f32[200,256]{1,0:T(8,128)S(1)} %collective-permute-done.15.refs_2_, f32[200,256]{1,0:T(8,128)S(1)} %collective-permute-done.16.refs_3_), custom_call_target="tpu_custom_call" | custom-call | tf_op jit(solution)/shard_map/pallas_call | solution.py:389
  43.7 1.8 %collective-permute-done.13.refs_3_ = f32[264,128]{1,0:T(8,128)S(1)} collective-permute-done((f32[264,128]{1,0:T(8,128)S(1)}, f32[264,128]{1,0:T(8,128)S(1)}, u32[]{:S(2)}, u32[]{:S(2)}) %collective-permute-start.13) | collective-permute-done | bytes 135200 | tf_op jit(solution)/shard_map/ppermute | solution.py:26
  45.5 7.9 %collective-permute-done.12.refs_2_ = f32[264,128]{1,0:T(8,128)S(1)} collective-permute-done((f32[264,128]{1,0:T(8,128)S(1)}, f32[264,128]{1,0:T(8,128)S(1)}, u32[]{:S(2)}, u32[]{:S(2)}) %collective-permute-start.12) | collective-permute-done | bytes 135200 | tf_op jit(solution)/shard_map/ppermute | solution.py:26
  53.5 1.0 %shard_map.65 = (f32[16,32,256]{2,1,0:T(8,128)}, f32[1,1]{1,0:T(1,128)}) custom-call(f32[264,128]{1,0:T(8,128)S(1)} %shard_map.64.refs_0_, f32[264,128]{1,0:T(8,128)S(1)} %collective-permute-done.11.refs_1_, f32[264,128]{1,0:T(8,128)S(1)} %collective-permute-done.12.refs_2_, f32[264,128]{1,0:T(8,128)S(1)} %collective-permute-done.13.refs_3_), custom_call_target="tpu_custom_call" | custom-call | tf_op jit(solution)/shard_map/pallas_call | solution.py:458
  (15 shorter events, 0.4 us)
Async XLA Ops:
  0.6 7.1 %collective-permute-start.3 = (f32[512,256]{1,0:T(8,128)}, f32[512,256]{1,0:T(8,128)S(1)}, u32[]{:S(2)}, u32[]{:S(2)}) collective-permute-start(f32[512,256]{1,0:T(8,128)} %bitcast.5), channel_id=1, source_target_pairs={{0,4},{4,0},{8,12},{12,8},{16,20},{20,16},{24,28},{28,24},{1,5},{5... | collective-permute-start | bytes 1572872 | tf_op jit(solution)/shard_map/ppermute | solution.py:26
  2.2 9.5 %collective-permute-start.2 = (f32[200,256]{1,0:T(8,128)S(1)}, f32[200,256]{1,0:T(8,128)S(1)}, u32[]{:S(2)}, u32[]{:S(2)}) collective-permute-start(f32[200,256]{1,0:T(8,128)S(1)} %shard_map.58.img_ref), channel_id=1, source_target_pairs={{0,24},{4,28},{8,16},{12,20},{16,8},{20,12},{24,0},{28,4},{1,25},{... | collective-permute-start | bytes 614408 | tf_op jit(solution)/shard_map/ppermute | solution.py:26
  5.7 10.1 %collective-permute-start.1 = (f32[200,256]{1,0:T(8,128)S(1)}, f32[200,256]{1,0:T(8,128)S(1)}, u32[]{:S(2)}, u32[]{:S(2)}) collective-permute-start(f32[200,256]{1,0:T(8,128)S(1)} %shard_map.58.img_ref), channel_id=1, source_target_pairs={{0,16},{4,20},{8,24},{12,28},{16,0},{20,4},{24,8},{28,12},{1,17},{... | collective-permute-start | bytes 614408 | tf_op jit(solution)/shard_map/ppermute | solution.py:26
  6.3 9.9 %collective-permute-start = (f32[200,256]{1,0:T(8,128)S(1)}, f32[200,256]{1,0:T(8,128)S(1)}, u32[]{:S(2)}, u32[]{:S(2)}) collective-permute-start(f32[200,256]{1,0:T(8,128)S(1)} %shard_map.58.img_ref), channel_id=1, source_target_pairs={{0,8},{4,12},{8,0},{12,4},{16,24},{20,28},{24,16},{28,20},{1,9},{5... | collective-permute-start | bytes 614408 | tf_op jit(solution)/shard_map/ppermute | solution.py:26
  19.8 2.0 %collective-permute-start.4 = (f32[1032,128]{1,0:T(8,128)S(1)}, f32[1032,128]{1,0:T(8,128)S(1)}, u32[]{:S(2)}, u32[]{:S(2)}) collective-permute-start(f32[1032,128]{1,0:T(8,128)S(1)} %get-tuple-element.35), channel_id=1, source_target_pairs={{0,4},{4,0},{8,12},{12,8},{16,20},{20,16},{24,28},{28,24},{1,5},{5... | collective-permute-start | bytes 1585160 | tf_op jit(solution)/shard_map/ppermute | solution.py:26
  19.9 22.7 %collective-permute-start.14 = (f32[200,256]{1,0:T(8,128)S(1)}, f32[200,256]{1,0:T(8,128)S(1)}, u32[]{:S(2)}, u32[]{:S(2)}) collective-permute-start(f32[200,256]{1,0:T(8,128)S(1)} %get-tuple-element.43), channel_id=1, source_target_pairs={{0,24},{4,28},{8,16},{12,20},{16,8},{20,12},{24,0},{28,4},{1,25},{... | collective-permute-start | bytes 614408 | tf_op jit(solution)/shard_map/ppermute | solution.py:26
  21.9 15.3 %collective-permute-start.5 = (f32[256,128]{1,0:T(8,128)S(1)}, f32[256,128]{1,0:T(8,128)S(1)}, u32[]{:S(2)}, u32[]{:S(2)}) collective-permute-start(f32[256,128]{1,0:T(8,128)S(1)} %get-tuple-element.37), channel_id=1, source_target_pairs={{0,1},{1,0},{2,3},{3,2},{4,5},{5,4},{6,7},{7,6},{8,9},{9,8},{10,11... | collective-permute-start | bytes 393224 | tf_op jit(solution)/shard_map/ppermute | solution.py:26
  23.6 5.5 %collective-permute-start.10 = (f32[8,128]{1,0:T(8,128)S(1)}, f32[8,128]{1,0:T(8,128)S(1)}, u32[]{:S(2)}, u32[]{:S(2)}) collective-permute-start(f32[8,128]{1,0:T(8,128)S(1)} %get-tuple-element.40.refs_4_), channel_id=1, source_target_pairs={{0,24},{4,28},{8,16},{12,20},{16,8},{20,12},{24,0},{28,4},{1,25},{... | collective-permute-start | bytes 12296 | tf_op jit(solution)/shard_map/ppermute | solution.py:26
  25.2 6.9 %collective-permute-start.9 = (f32[8,128]{1,0:T(8,128)S(1)}, f32[8,128]{1,0:T(8,128)S(1)}, u32[]{:S(2)}, u32[]{:S(2)}) collective-permute-start(f32[8,128]{1,0:T(8,128)S(1)} %get-tuple-element.40.refs_4_), channel_id=1, source_target_pairs={{0,16},{4,20},{8,24},{12,28},{16,0},{20,4},{24,8},{28,12},{1,17},{... | collective-permute-start | bytes 12296 | tf_op jit(solution)/shard_map/ppermute | solution.py:26
  26.5 11.5 %collective-permute-start.6 = (f32[256,128]{1,0:T(8,128)S(1)}, f32[256,128]{1,0:T(8,128)S(1)}, u32[]{:S(2)}, u32[]{:S(2)}) collective-permute-start(f32[256,128]{1,0:T(8,128)S(1)} %get-tuple-element.38), channel_id=1, source_target_pairs={{0,2},{1,3},{2,0},{3,1},{4,6},{5,7},{6,4},{7,5},{8,10},{9,11},{10,... | collective-permute-start | bytes 393224 | tf_op jit(solution)/shard_map/ppermute | solution.py:26
  29.1 9.0 %collective-permute-start.7 = (f32[256,128]{1,0:T(8,128)S(1)}, f32[256,128]{1,0:T(8,128)S(1)}, u32[]{:S(2)}, u32[]{:S(2)}) collective-permute-start(f32[256,128]{1,0:T(8,128)S(1)} %get-tuple-element.39), channel_id=1, source_target_pairs={{0,3},{1,2},{2,1},{3,0},{4,7},{5,6},{6,5},{7,4},{8,11},{9,10},{10,... | collective-permute-start | bytes 393224 | tf_op jit(solution)/shard_map/ppermute | solution.py:26
  32.1 3.6 %collective-permute-start.8 = (f32[8,128]{1,0:T(8,128)S(1)}, f32[8,128]{1,0:T(8,128)S(1)}, u32[]{:S(2)}, u32[]{:S(2)}) collective-permute-start(f32[8,128]{1,0:T(8,128)S(1)} %get-tuple-element.40.refs_4_), channel_id=1, source_target_pairs={{0,8},{4,12},{8,0},{12,4},{16,24},{20,28},{24,16},{28,20},{1,9},{5... | collective-permute-start | bytes 12296 | tf_op jit(solution)/shard_map/ppermute | solution.py:26
  35.7 7.1 %collective-permute-start.15 = (f32[200,256]{1,0:T(8,128)S(1)}, f32[200,256]{1,0:T(8,128)S(1)}, u32[]{:S(2)}, u32[]{:S(2)}) collective-permute-start(f32[200,256]{1,0:T(8,128)S(1)} %get-tuple-element.48), channel_id=1, source_target_pairs={{0,8},{4,12},{8,0},{12,4},{16,24},{20,28},{24,16},{28,20},{1,9},{5... | collective-permute-start | bytes 614408 | tf_op jit(solution)/shard_map/ppermute | solution.py:26
  37.2 5.8 %collective-permute-start.16 = (f32[200,256]{1,0:T(8,128)S(1)}, f32[200,256]{1,0:T(8,128)S(1)}, u32[]{:S(2)}, u32[]{:S(2)}) collective-permute-start(f32[200,256]{1,0:T(8,128)S(1)} %get-tuple-element.49), channel_id=1, source_target_pairs={{0,16},{4,20},{8,24},{12,28},{16,0},{20,4},{24,8},{28,12},{1,17},{... | collective-permute-start | bytes 614408 | tf_op jit(solution)/shard_map/ppermute | solution.py:26
  38.1 7.4 %collective-permute-start.13 = (f32[264,128]{1,0:T(8,128)S(1)}, f32[264,128]{1,0:T(8,128)S(1)}, u32[]{:S(2)}, u32[]{:S(2)}) collective-permute-start(f32[264,128]{1,0:T(8,128)S(1)} %shard_map.64.refs_0_), channel_id=1, source_target_pairs={{0,3},{1,2},{2,1},{3,0},{4,7},{5,6},{6,5},{7,4},{8,11},{9,10},{10,... | collective-permute-start | bytes 405512 | tf_op jit(solution)/shard_map/ppermute | solution.py:26
  41.4 12.1 %collective-permute-start.12 = (f32[264,128]{1,0:T(8,128)S(1)}, f32[264,128]{1,0:T(8,128)S(1)}, u32[]{:S(2)}, u32[]{:S(2)}) collective-permute-start(f32[264,128]{1,0:T(8,128)S(1)} %shard_map.64.refs_0_), channel_id=1, source_target_pairs={{0,2},{1,3},{2,0},{3,1},{4,6},{5,7},{6,4},{7,5},{8,10},{9,11},{10,... | collective-permute-start | bytes 405512 | tf_op jit(solution)/shard_map/ppermute | solution.py:26
  42.6 10.9 %collective-permute-start.11 = (f32[264,128]{1,0:T(8,128)S(1)}, f32[264,128]{1,0:T(8,128)S(1)}, u32[]{:S(2)}, u32[]{:S(2)}) collective-permute-start(f32[264,128]{1,0:T(8,128)S(1)} %shard_map.64.refs_0_), channel_id=1, source_target_pairs={{0,1},{1,0},{2,3},{3,2},{4,5},{5,4},{6,7},{7,6},{8,9},{9,8},{10,11... | collective-permute-start | bytes 405512 | tf_op jit(solution)/shard_map/ppermute | solution.py:26
